TPU v7x, 32 devices: a whole 2x2x4 slice. The times are simulated.
32 devices in a mesh: row: 4 (over y, x), col: 8 (over z, core).
Axes of the slice: x: 2, y: 2, z: 4, core: 2. Of those that a mesh axis runs over, the one named last changes fastest.
Arguments:
- cam_jac: bfloat16 [2, 2, 6, 512, 1024], P(None, None, None, ('row', 'col')), may hold values from -0.09375 to 0.09375
- pt_jac: bfloat16 [2, 2, 3, 512, 1024], P(None, None, None, ('row', 'col')), may hold values from -6 to 6
- resid: bfloat16 [2, 2, 512, 1024], P(None, None, ('row', 'col')), may hold values from -6 to 6
- partner: int32 [512, 1024], P(('row', 'col')), may hold values from 0 to 511, as said below
- count: int32 [512], P(('row', 'col')), may hold values from 512 to 1024
- tile_map: int32 [512], replicated, may hold values from 0 to 511, as said below
Outputs:
- coupling: bfloat16 [6, 6, 512, 512], P(None, None, 'row', 'col')
- camera_update: float32 [6, 512], P(None, 'row')
- residual: float32 [6, 512], P(None, 'row')
Inputs may be any that keep to these rules, and one draw needn't show every extreme that they name: partner[a, t] is never a. `tile_map`: a permutation of the tile positions; of the 16 consecutive scenes of each device, exactly 4 have positions in each block of 128 consecutive positions.
All inputs are finite; a program needn't handle non-finite values.
Results may differ from a plain program's by a relative error of at most 0.0015.
Values may be sent and summed in bfloat16 or wider, within the bound.
No kernel may reach another device: no remote copies, remote signals or barrier semaphores. Data moves between devices by JAX's collectives and lax.ppermute only.
A program may use at most 64 MiB of HBM per device.

v0:
```python
import jax
import jax.numpy as jnp
from jax import lax
from jax.sharding import PartitionSpec as P

ITERS = 3


CAMERA_DAMPING = 1.0
POINT_DAMPING = 1.0


def cross_product(first_vec, second_vec):
    return jnp.stack(
        [
            first_vec[1] * second_vec[2] - first_vec[2] * second_vec[1],
            first_vec[2] * second_vec[0] - first_vec[0] * second_vec[2],
            first_vec[0] * second_vec[1] - first_vec[1] * second_vec[0],
        ],
        axis=0,
    )


def point_terms(camera, points_jac, errors):
    camera = camera.astype(jnp.float32)
    points_jac = points_jac.astype(jnp.float32)
    errors = errors.astype(jnp.float32)
    own_jac, other_jac = (camera[0], camera[1])
    own_point, other_point = (points_jac[0], points_jac[1])
    own_error, other_error = (errors[0], errors[1])
    point_hessian = jnp.sum(own_point[:, :, None] * own_point[:, None, :], axis=0)
    point_hessian = point_hessian + jnp.sum(
        other_point[:, :, None] * other_point[:, None, :], axis=0
    )
    point_hessian = point_hessian + POINT_DAMPING * jnp.eye(3, dtype=jnp.float32)[:, :, None, None]
    first_row, second_row, third_row = (point_hessian[0], point_hessian[1], point_hessian[2])
    cofactor_first = cross_product(second_row, third_row)
    cofactor_second = cross_product(third_row, first_row)
    cofactor_third = cross_product(first_row, second_row)
    determinant = jnp.sum(first_row * cofactor_first, axis=0)
    inverse = jnp.stack([cofactor_first, cofactor_second, cofactor_third], axis=1) / determinant
    w_own = jnp.sum(own_jac[:, :, None] * own_point[:, None, :], axis=0)
    w_other = jnp.sum(other_jac[:, :, None] * other_point[:, None, :], axis=0)
    point_rhs = -(
        jnp.sum(own_point * own_error[:, None], axis=0)
        + jnp.sum(other_point * other_error[:, None], axis=0)
    )
    own_vi = jnp.sum(w_own[:, :, None] * inverse[None, :, :], axis=1)
    other_vi = jnp.sum(w_other[:, :, None] * inverse[None, :, :], axis=1)
    diag_own = jnp.sum(own_jac[:, :, None] * own_jac[:, None, :], axis=0) - jnp.sum(
        own_vi[:, None, :] * w_own[None, :, :], axis=2
    )
    diag_other = jnp.sum(other_jac[:, :, None] * other_jac[:, None, :], axis=0) - jnp.sum(
        other_vi[:, None, :] * w_other[None, :, :], axis=2
    )
    link = -jnp.sum(own_vi[:, None, :] * w_other[None, :, :], axis=2)
    grad_own = -jnp.sum(own_jac * own_error[:, None], axis=0) - jnp.sum(
        own_vi * point_rhs[None], axis=1
    )
    grad_other = -jnp.sum(other_jac * other_error[:, None], axis=0) - jnp.sum(
        other_vi * point_rhs[None], axis=1
    )
    return (diag_own, diag_other, link, grad_own, grad_other)


def conjugate_steps(right_side, apply_operator, inner_product):
    solution = jnp.zeros_like(right_side)
    remainder = right_side
    direction = right_side
    norm_now = inner_product(remainder, remainder)
    for iteration in range(ITERS):
        product_vec = apply_operator(direction)
        step_size = norm_now / inner_product(direction, product_vec)
        solution = solution + step_size * direction
        remainder = remainder - step_size * product_vec
        norm_next = inner_product(remainder, remainder)
        direction = remainder + norm_next / norm_now * direction
        norm_now = norm_next
    return (solution, remainder)


def shards(cam_jac, pt_jac, resid, partner, count, tile_map):
    row_count = lax.axis_size("row")
    col_count = lax.axis_size("col")
    scenes = tile_map.shape[0]
    scn_local = partner.shape[0]
    points = partner.shape[1]
    tile_rows = scenes // row_count
    tile_cols = scenes // col_count
    per_group = scn_local // row_count
    row_index = lax.axis_index("row")
    col_index = lax.axis_index("col")
    device = row_index * col_count + col_index
    positions = jnp.arange(scenes, dtype=jnp.int32)
    tile_own = lax.dynamic_slice_in_dim(tile_map, device * scn_local, scn_local)
    local_rank = jnp.sum((tile_own[None, :] < tile_own[:, None]).astype(jnp.int32), axis=1)
    active = (jnp.arange(points, dtype=jnp.int32)[None, :] < count[:, None]).astype(jnp.float32)
    diag_own, diag_other, link, grad_own, grad_other = point_terms(cam_jac, pt_jac, resid)
    values = (
        jnp.concatenate(
            [
                link.reshape(36, scn_local, points),
                diag_other.reshape(36, scn_local, points),
                grad_other,
            ],
            axis=0,
        )
        * active[None]
    )
    values = jnp.moveaxis(values, 1, 0)

    def scene_sums(item):
        scene_values, scene_partner = item
        hits = scene_partner[:, None] == positions[None, :]
        tile_other = jnp.sum(jnp.where(hits, tile_map[None, :], 0), axis=1)
        onehot = (tile_other[:, None] == positions[None, :]).astype(jnp.float32)
        return jnp.dot(
            scene_values,
            onehot,
            precision=lax.Precision.HIGHEST,
            preferred_element_type=jnp.float32,
        )

    per_scene = lax.map(scene_sums, (values, partner))
    link_rows = per_scene[:, :36, :]
    other_sum = jnp.sum(per_scene[:, 36:, :], axis=0)
    ordering = (local_rank[None, :] == jnp.arange(scn_local, dtype=jnp.int32)[:, None]).astype(
        jnp.float32
    )
    panel = jnp.einsum("rs,sxc->xrc", ordering, link_rows, precision=lax.Precision.HIGHEST)
    panel = panel.reshape(36, row_count, per_group, col_count, tile_cols).transpose(0, 1, 3, 2, 4)
    panel_short = panel.astype(jnp.bfloat16)
    own_onehot = (tile_own[:, None] == positions[None, :]).astype(jnp.float32)
    own_diag = jnp.sum(diag_own * active, axis=-1).reshape(36, scn_local)
    own_grad = jnp.sum(grad_own * active, axis=-1)
    own_both = jnp.concatenate([own_diag, own_grad], axis=0)
    own_spread = jnp.dot(
        own_both, own_onehot, precision=lax.Precision.HIGHEST, preferred_element_type=jnp.float32
    )
    both_part = own_spread + other_sum
    diag_part = both_part[:36]
    grad_part = both_part[36:]
    shaped = panel_short.reshape(36, row_count * col_count, per_group, tile_cols)
    received = lax.all_to_all(shaped, ("row", "col"), split_axis=1, concat_axis=1, tiled=True)
    received = received.reshape(36, tile_rows, tile_cols)
    diag_all, grad_all = lax.psum((diag_part, grad_part), ("row", "col"))
    row_start = row_index * tile_rows
    col_start = col_index * tile_cols
    devices = scenes // scn_local
    tiles_grid = tile_map.reshape(devices, scn_local)
    inblock = (tiles_grid >= row_start) & (tiles_grid < row_start + tile_rows)
    lower = (tiles_grid[:, None, :] < tiles_grid[:, :, None]) & inblock[:, None, :]
    within_all = jnp.sum(lower.astype(jnp.int32), axis=2)
    slot_from = (jnp.arange(devices, dtype=jnp.int32)[:, None] * per_group + within_all).reshape(-1)
    slot_to = (tiles_grid - row_start).reshape(-1)
    slots = jnp.arange(tile_rows, dtype=jnp.int32)
    to_table = ((slot_to[:, None] == slots[None, :]) & inblock.reshape(-1)[:, None]).astype(
        jnp.bfloat16
    )
    from_table = (slot_from[:, None] == slots[None, :]).astype(jnp.bfloat16)
    selection = jnp.dot(to_table.T, from_table, preferred_element_type=jnp.float32).astype(
        jnp.bfloat16
    )
    coupling_tile = jnp.einsum(
        "pk,xkc->xpc", selection, received, preferred_element_type=jnp.float32
    )
    coupling_tile = coupling_tile.astype(jnp.bfloat16).reshape(6, 6, tile_rows, tile_cols)
    coupling_wide = coupling_tile.astype(jnp.float32)
    zero_at = row_index * 0

    def tile_products(rows_part, cols_part):
        forward = jnp.einsum(
            "xyij,yj->xi", coupling_wide, cols_part, precision=lax.Precision.HIGHEST
        )
        backward = jnp.einsum(
            "xyij,xi->yj", coupling_wide, rows_part, precision=lax.Precision.HIGHEST
        )
        empty = jnp.zeros((6, scenes), jnp.float32)
        spread = lax.dynamic_update_slice(empty, forward, (zero_at, row_start))
        spread = spread + lax.dynamic_update_slice(empty, backward, (zero_at, col_start))
        return lax.psum(spread, ("row", "col"))

    diag_blocks = diag_all.reshape(6, 6, scenes)

    def apply_full(direction):
        rows_part = lax.dynamic_slice_in_dim(direction, row_start, tile_rows, 1)
        cols_part = lax.dynamic_slice_in_dim(direction, col_start, tile_cols, 1)
        summed = tile_products(rows_part, cols_part)
        result = CAMERA_DAMPING * direction
        result = result + jnp.einsum(
            "xyi,yi->xi", diag_blocks, direction, precision=lax.Precision.HIGHEST
        )
        return result + summed

    def inner_full(first_vec, second_vec):
        return jnp.sum(first_vec * second_vec)

    whole_solution, whole_remainder = conjugate_steps(grad_all, apply_full, inner_full)
    solution = lax.dynamic_slice_in_dim(whole_solution, row_start, tile_rows, 1)
    remainder = lax.dynamic_slice_in_dim(whole_remainder, row_start, tile_rows, 1)
    return (coupling_tile, solution, remainder)


def solution(mesh):
    return jax.shard_map(
        shards,
        mesh=mesh,
        in_specs=(
            P(None, None, None, ("row", "col"), None),
            P(None, None, None, ("row", "col"), None),
            P(None, None, ("row", "col"), None),
            P(("row", "col"), None),
            P(("row", "col")),
            P(),
        ),
        out_specs=(P(None, None, "row", "col"), P(None, "row"), P(None, "row")),
        check_vma=False,
    )
```

profile of v0, /device:TPU:0, one launch (start us, length us, event | category | flops | bytes accessed | tf_op | source)
XLA Modules:
  0.0 395.3 jit_solution(5437719041077850212)
XLA Ops:
  13.1 2.9 multiply_reduce_fusion.8
  16.1 2.6 multiply_reduce_fusion.3
  23.3 6.3 %multiply_reduce_fusion = (f32[6,6,16,1024]{3,2,1,0:T(8,128)}, f32[6,6,16,1024]{3,2,1,0:T(8,128)}, f32[6,6,16,1024]{3,2,1,0:T(8,128)}) fusion(f32[6,3,16,1024]{3,2,1,0:T(8,128)S(1)} %copy-done.1, f32[6,3,16,1024]{3,2,1,0:T(8,128)S(1)} %get-tuple-element.89, f32[6,3,16,1024]{3,2,1,0:T(8,128)S(1)} %get-tuple-element.127, ...), kind=kLoop, calls=%fused_computation.11 | loop fusion | flops 8847360 | bytes 11796480 | tf_op jit(solution)/shard_map/reduce_sum | solution.py:50
  30.8 2.0 neg.20
  35.0 2.8 sub.170
  37.8 2.8 fusion.6
  40.6 78.3 %while.12 = (s32[]{:T(128)}, f32[16,78,512]{2,1,0:T(8,128)}, f32[16,78,1024]{2,0,1:T(8,128)}, s32[16,1024]{1,0:T(8,128)}, s32[512]{0:T(512)S(1)}, /*index=5*/s32[]{:T(128)}) while((s32[]{:T(128)}, f32[16,78,512]{2,1,0:T(8,128)}, f32[16,78,1024]{2,0,1:T(8,128)}, s32[16,1024]{1,0:T(8,128)}, s32[512]{0:T(512)S(1)}, ...), condition=%wide.region_16.0_spmd.clone.clone, body=%wide.region_14.16_spmd.clone.clone.sunk | while | flops 492829696 | bytes 1144921 | solution.py:124
  41.9 2.0 constant_dynamic-slice_fusion.5
  46.8 2.0 constant_dynamic-slice_fusion.5
  51.6 2.0 constant_dynamic-slice_fusion.5
  56.5 2.0 constant_dynamic-slice_fusion.5
  61.4 2.0 constant_dynamic-slice_fusion.5
  66.3 2.0 constant_dynamic-slice_fusion.5
  81.0 2.0 constant_dynamic-slice_fusion.5
  90.8 2.0 constant_dynamic-slice_fusion.5
  95.7 2.0 constant_dynamic-slice_fusion.5
  105.5 2.0 constant_dynamic-slice_fusion.5
  121.8 2.7 fusion.12
  127.4 7.3 %all-to-all-start = ((bf16[32,2,4608]{2,1,0:T(2,128)(2,1)}), bf16[32,2,4608]{2,1,0:T(2,128)(2,1)S(1)}, u32[]{:S(2)}, u32[]{:S(2)}) async-start(bf16[32,2,4608]{2,1,0:T(2,128)(2,1)} %reshape.571), calls=%async_computation | async-start | bytes 1179648 | tf_op jit(solution)/shard_map/all_to_all | solution.py:144
  135.0 41.1 %psum.35 = f32[6,512]{1,0:T(8,128)S(1)} all-reduce(f32[6,512]{1,0:T(8,128)S(1)} %slice.143), channel_id=1, replica_groups=mesh['row'=4,'col'=8] {'row','col'}, use_global_device_ids=true, to_apply=%region_26.27 | all-reduce | flops 3072 | bytes 24576 | tf_op jit(solution)/shard_map/psum | solution.py:146
  176.4 71.8 %all-reduce.2.cloned.1.call-done = f32[6,6,512]{2,1,0:T(8,128)} async-done(((f32[6,6,512]{2,1,0:T(8,128)}), f32[6,6,512]{2,1,0:T(8,128)}) %all-reduce.2.cloned.1.call-update) | async-done | bytes 73744 | tf_op jit(solution)/shard_map/psum | solution.py:146
  252.8 41.2 %psum.37 = f32[6,512]{1,0:T(8,128)S(1)} all-reduce(f32[6,512]{1,0:T(8,128)S(1)} %add.132), channel_id=1, replica_groups=mesh['row'=4,'col'=8] {'row','col'}, use_global_device_ids=true, to_apply=%region_29.30 | all-reduce | flops 3072 | bytes 24576 | tf_op jit(solution)/shard_map/psum | solution.py:181
  299.6 40.0 %psum.38 = f32[6,512]{1,0:T(8,128)S(1)} all-reduce(f32[6,512]{1,0:T(8,128)S(1)} %add.136), channel_id=1, replica_groups=mesh['row'=4,'col'=8] {'row','col'}, use_global_device_ids=true, to_apply=%region_32.33 | all-reduce | flops 3072 | bytes 24576 | tf_op jit(solution)/shard_map/psum | solution.py:181
  345.2 40.1 %psum.39 = f32[6,512]{1,0:T(8,128)S(1)} all-reduce(f32[6,512]{1,0:T(8,128)S(1)} %add.141), channel_id=1, replica_groups=mesh['row'=4,'col'=8] {'row','col'}, use_global_device_ids=true, to_apply=%region_35.36 | all-reduce | flops 3072 | bytes 24576 | tf_op jit(solution)/shard_map/psum | solution.py:181
  (172 shorter events, 90.0 us)
Async XLA Ops:
  7.2 241.0 %all-reduce.2.cloned.1.call-start = ((), (), s32[]{:S(2)}) async-start(), calls=%async_computation.1 | async-start | bytes 196608 | tf_op jit(solution)/shard_map/psum | solution.py:146
  8.4 0.7 copy-start.4
  8.4 0.9 copy-start.5
  8.6 2.1 copy-start.10
  8.6 2.1 copy-start.9
  16.1 2.6 copy-start.12
  18.7 3.9 copy-start.1
  29.6 1.0 copy-start.7
  30.8 2.4 copy-start.2
  30.8 3.1 copy-start.3
  33.9 0.7 copy-start.11
  33.9 1.0 copy-start.6
  127.4 121.7 %all-to-all-start = ((bf16[32,2,4608]{2,1,0:T(2,128)(2,1)}), bf16[32,2,4608]{2,1,0:T(2,128)(2,1)S(1)}, u32[]{:S(2)}, u32[]{:S(2)}) async-start(bf16[32,2,4608]{2,1,0:T(2,128)(2,1)} %reshape.571), calls=%async_computation | async-start | bytes 1179648 | tf_op jit(solution)/shard_map/all_to_all | solution.py:144
  250.5 89.1 %copy-start.8 = (f32[6,6,512]{2,1,0:T(8,128)S(1)}, f32[6,6,512]{2,1,0:T(8,128)}, u32[]{:S(2)}) copy-start(f32[6,6,512]{2,1,0:T(8,128)} %all-reduce.2.cloned.1.call-done) | copy-start | bytes 221188
  251.3 137.2 %copy-start = (bf16[36,64,128]{2,1,0:T(8,128)(2,1)}, bf16[36,64,128]{2,1,0:T(8,128)(2,1)S(1)}, u32[]{:S(2)}) copy-start(bf16[36,64,128]{2,1,0:T(8,128)(2,1)S(1)} %convolution_convert_fusion) | copy-start | bytes 1769476
Sparse Core Ops, SparseCore 0:
  121.7 126.4 all-reduce.1
where the time goes:
time: 398 us; the launch traced here: 395 us
  blocking collectives  162 us (41%)
  waiting for transfers between devices  71.8 us (18%)
  local copies, waits for them, and re-layouts  53.9 us (14%)
  other arithmetic  44.9 us (11%)
  matrix products  33.6 us (8%)
  between operations  21.2 us (5%)
  starting transfers between devices  7.36 us (2%)
    psum x3, blocking collectives, tile_products(): return lax.psum(spread, ('row', 'col'))  121 us
    psum x1, waiting for transfers between devices, shards(): diag_all, grad_all = lax.psum((diag_part, grad_part), ('row', 'col'))  71.8 us
    dynamic_slice x32, local copies, waits for them, and re-layouts, shards(): per_scene = lax.map(scene_sums, (values, partner))  44.5 us
    psum x1, blocking collectives, shards(): diag_all, grad_all = lax.psum((diag_part, grad_part), ('row', 'col'))  41.1 us
    dot_general x16, matrix products, scene_sums(): jnp.dot(scene_values, onehot, precision=lax.Precision.HIGHEST, preferred_...  26.2 us
  transfers between devices with their start and end apart: 2, of which 1 were waited for; matrix products, arithmetic and copies ran while one was open for 2% of the time, Pallas kernels for 0%

commit v1 on v0

--- a/solution.py
+++ b/solution.py
@@ -1,13 +1,521 @@
 import jax
 import jax.numpy as jnp
 from jax import lax
+from jax.experimental import pallas as pl
+from jax.experimental.pallas import tpu as pltpu
 from jax.sharding import PartitionSpec as P
 
 ITERS = 3
-
-
 CAMERA_DAMPING = 1.0
 POINT_DAMPING = 1.0
+AXES = ("row", "col")
+LANES = 128
+HALF = 64
+F32 = jnp.float32
+BF16 = jnp.bfloat16
+PAIRS = [(x, y) for x in range(6) for y in range(x, 6)]
+CONTRACT_LAST = (((1,), (1,)), ((), ()))
+
+
+def iota(shape, dim):
+    return lax.broadcasted_iota(jnp.int32, shape, dim)
+
+
+def split_two(value):
+    high = value.astype(BF16)
+    low = (value - high.astype(F32)).astype(BF16)
+    return high, low
+
+
+def dot2(left, right):
+    a, b = left
+    c, d = right
+    return a * c + b * d
+
+
+def point_values(ja, jb, pa, pb, ea, eb, live):
+    one = POINT_DAMPING
+    hess = {}
+    for x in range(3):
+        for y in range(x, 3):
+            h = pa[0][x] * pa[0][y] + pa[1][x] * pa[1][y]
+            h = h + (pb[0][x] * pb[0][y] + pb[1][x] * pb[1][y])
+            hess[x, y] = h + one if x == y else h
+    a, b, c = hess[0, 0], hess[0, 1], hess[0, 2]
+    d, e, f = hess[1, 1], hess[1, 2], hess[2, 2]
+    c00 = d * f - e * e
+    c01 = c * e - b * f
+    c02 = b * e - c * d
+    c11 = a * f - c * c
+    c12 = b * c - a * e
+    c22 = a * d - b * b
+    det = a * c00 + b * c01 + c * c02
+    inv = 1.0 / det
+    vi = [[c00 * inv, c01 * inv, c02 * inv], [None, c11 * inv, c12 * inv], [None, None, c22 * inv]]
+    vi[1][0], vi[2][0], vi[2][1] = vi[0][1], vi[0][2], vi[1][2]
+    q = [
+        -((pa[0][k] * ea[0] + pa[1][k] * ea[1]) + (pb[0][k] * eb[0] + pb[1][k] * eb[1]))
+        for k in range(3)
+    ]
+    viq = [vi[k][0] * q[0] + vi[k][1] * q[1] + vi[k][2] * q[2] for k in range(3)]
+
+    def times_vi(p):
+        return [
+            [p[m][0] * vi[0][k] + p[m][1] * vi[1][k] + p[m][2] * vi[2][k] for k in range(3)]
+            for m in range(2)
+        ]
+
+    def inner(left, right):
+        return left[0] * right[0] + left[1] * right[1] + left[2] * right[2]
+
+    def keep(value):
+        return jnp.where(live, value, 0.0)
+
+    av = times_vi(pa)
+    bv = times_vi(pb)
+    m_ab = [[keep(-inner(av[m], pb[k])) for k in range(2)] for m in range(2)]
+    g_aa = [keep(1.0 - inner(av[0], pa[0])), keep(-inner(av[0], pa[1])), keep(1.0 - inner(av[1], pa[1]))]
+    g_bb = [keep(1.0 - inner(bv[0], pb[0])), keep(-inner(bv[0], pb[1])), keep(1.0 - inner(bv[1], pb[1]))]
+    h_a = [keep(-(ea[m] + inner(pa[m], viq))) for m in range(2)]
+    h_b = [keep(-(eb[m] + inner(pb[m], viq))) for m in range(2)]
+
+    mj = [[m_ab[m][0] * jb[0][y] + m_ab[m][1] * jb[1][y] for y in range(6)] for m in range(2)]
+    link = {}
+    for x in range(6):
+        for y in range(6):
+            link[x, y] = ja[0][x] * mj[0][y] + ja[1][x] * mj[1][y]
+
+    def diagonal(j, g):
+        gj = [
+            [g[0] * j[0][y] + g[1] * j[1][y] for y in range(6)],
+            [g[1] * j[0][y] + g[2] * j[1][y] for y in range(6)],
+        ]
+        return [j[0][x] * gj[0][y] + j[1][x] * gj[1][y] for x, y in PAIRS]
+
+    diag_own = diagonal(ja, g_aa)
+    diag_other = diagonal(jb, g_bb)
+    grad_own = [ja[0][x] * h_a[0] + ja[1][x] * h_a[1] for x in range(6)]
+    grad_other = [jb[0][x] * h_b[0] + jb[1][x] * h_b[1] for x in range(6)]
+    return diag_own, diag_other, link, grad_own, grad_other
+
+
+def assemble_kernel(
+    row_count, col_count, cam_ref, pt_ref, res_ref, partner_ref, map_ref, count_sm, map_sm, send_ref,
+    vals_ref, own_ref, acc_ref, links_ref, flat_ref, extra_ref, perm_ref,
+):
+    scn = partner_ref.shape[0]
+    points = partner_ref.shape[1]
+    scenes = map_ref.shape[1]
+    per_group = scn // row_count
+    device = lax.axis_index("row") * col_count + lax.axis_index("col")
+    slab = (scn, LANES)
+
+    sub = iota(slab, 0)
+    counts = jnp.zeros(slab, jnp.int32)
+    for s in range(scn):
+        counts = jnp.where(sub == s, count_sm[s], counts)
+    own_ref[...] = jnp.zeros_like(own_ref)
+    acc_ref[...] = jnp.zeros_like(acc_ref)
+    vals_ref[:, pl.ds(63 * scn, scn), :] = jnp.zeros((points // LANES, scn, LANES), F32)
+
+    def slab_step(step, carry):
+        lanes = pl.ds(pl.multiple_of(step * LANES, LANES), LANES)
+
+        def get(ref, *where):
+            return ref[where + (slice(None), lanes)].astype(F32)
+
+        ja = [[get(cam_ref, 0, m, x) for x in range(6)] for m in range(2)]
+        jb = [[get(cam_ref, 1, m, x) for x in range(6)] for m in range(2)]
+        pa = [[get(pt_ref, 0, m, x) for x in range(3)] for m in range(2)]
+        pb = [[get(pt_ref, 1, m, x) for x in range(3)] for m in range(2)]
+        ea = [get(res_ref, 0, m) for m in range(2)]
+        eb = [get(res_ref, 1, m) for m in range(2)]
+        live = (iota(slab, 1) + step * LANES) < counts
+        diag_own, diag_other, link, grad_own, grad_other = point_values(ja, jb, pa, pb, ea, eb, live)
+
+        def put(q, value):
+            vals_ref[step, pl.ds(q * scn, scn), :] = value
+
+        def put_own(q, value):
+            own_ref[pl.ds(q * scn, scn), :] += value
+
+        for x in range(3):
+            for y in range(6):
+                put(x * 6 + y, link[x, y])
+                put(24 + x * 6 + y, link[x + 3, y])
+        for x in range(6):
+            put(18 + x, grad_other[x])
+            put_own(2 + x, grad_own[x])
+        for q in range(21):
+            put(42 + q, diag_other[q])
+            put_own(10 + q, diag_own[q])
+        return carry
+
+    lax.fori_loop(0, points // LANES, slab_step, 0)
+
+    spots = iota((scenes, points), 0)
+
+    def scene_step(s, carry):
+        values = jnp.concatenate(
+            [vals_ref.at[t][pl.ds(s, 64, stride=scn), :] for t in range(points // LANES)], axis=1
+        )
+        high, low = split_two(values)
+        left = jnp.concatenate([high, low], axis=0)
+        onehot = jnp.where(spots == partner_ref[pl.ds(s, 1), :], 1.0, 0.0).astype(BF16)
+        both = lax.dot_general(left, onehot, CONTRACT_LAST, preferred_element_type=F32)
+        total = both[:64] + both[64:]
+        acc_ref[...] += total
+        mine = map_sm[device * scn + s]
+        rank = jnp.int32(0)
+        for other in range(scn):
+            rank = rank + (map_sm[device * scn + other] < mine).astype(jnp.int32)
+        links_ref[pl.ds(pl.multiple_of(rank * 48, 16), 48), :] = total[:48].astype(BF16)
+        return carry
+
+    lax.fori_loop(0, scn, scene_step, 0)
+
+    lane = iota((32, LANES), 1)
+    own = jnp.zeros((32, LANES), F32)
+    for s in range(scn):
+        column = jnp.sum(own_ref[pl.ds(s, 32, stride=scn), :], axis=1, keepdims=True)
+        own = own + jnp.where(lane == s, column, 0.0)
+    start = device * scn
+    own = pltpu.roll(own, lax.rem(start, LANES), 1)
+    tile_at = lax.div(start, LANES)
+    for t in range(scenes // LANES):
+        cols = pl.ds(t * LANES, LANES)
+        whole = jnp.concatenate([acc_ref[16:24, cols], acc_ref[40:64, cols]], axis=0)
+        whole = whole + jnp.where(tile_at == t, own, 0.0)
+        high, low = split_two(whole)
+        flat_ref[0:32, cols] = high.astype(F32)
+        flat_ref[32:64, cols] = low.astype(F32)
+    per_col = -(-21 // col_count)
+    extra_ref[...] = jnp.zeros_like(extra_ref)
+    for c in range(col_count):
+        for i in range(per_col):
+            q = c * per_col + i
+            if q < 21:
+                extra_ref[c * 8 + 2 + i : c * 8 + 3 + i, :] = flat_ref[10 + q : 11 + q, :]
+                extra_ref[c * 8 + 5 + i : c * 8 + 6 + i, :] = flat_ref[42 + q : 43 + q, :]
+    base = col_count * 8
+    extra_ref[base : base + 8, :] = flat_ref[0:8, :]
+    extra_ref[base + 8 : base + 16, :] = flat_ref[32:40, :]
+
+    onto = jnp.where(iota((scenes, scenes), 0) == map_ref[...], 1.0, 0.0).astype(BF16)
+    left = jnp.concatenate([links_ref[...], extra_ref[...].astype(BF16)], axis=0)
+    perm_ref[...] = lax.dot_general(left, onto, CONTRACT_LAST, preferred_element_type=F32)
+
+    top = scn * 48
+    first = iota((8, LANES), 1) < HALF
+    keep_rows = iota((8, LANES), 0) < 2
+    first24 = iota((24, LANES), 1) < HALF
+
+    def merge(low_part, high_part, mask):
+        even = jnp.where(mask, low_part, pltpu.roll(high_part, HALF, 1))
+        odd = jnp.where(mask, pltpu.roll(low_part, HALF, 1), high_part)
+        return even, odd
+
+    for j in range(col_count // 2):
+        cols = pl.ds(j * LANES, LANES)
+        grad_cols = merge(
+            perm_ref[top + base : top + base + 8, cols],
+            perm_ref[top + base + 8 : top + base + 16, cols],
+            first,
+        )
+        for r in range(row_count):
+            rows = pl.ds(r * LANES, LANES)
+            grad_high = perm_ref[top + base : top + base + 8, rows]
+            grad_low = perm_ref[top + base + 8 : top + base + 16, rows]
+            for slot in range(per_group):
+                at = (r * per_group + slot) * 48
+                pieces = merge(perm_ref[at : at + 24, cols], perm_ref[at + 24 : at + 48, cols], first24)
+                for k in range(2):
+                    c = 2 * j + k
+                    if slot == 0:
+                        extra = grad_high
+                    elif slot == 1:
+                        extra = grad_low
+                    elif slot == 2:
+                        extra = grad_cols[k]
+                    else:
+                        extra = perm_ref[top + c * 8 : top + c * 8 + 8, rows]
+                    tail = jnp.where(keep_rows, pieces[k][16:24], extra)
+                    block = jnp.concatenate([pieces[k][0:16], tail], axis=0)
+                    send_ref[r * col_count + c, slot * 24 : slot * 24 + 24, :] = block.astype(BF16)
+
+
+def exact_dot(left, right, dims):
+    return lax.dot_general(
+        left, right, dims, precision=lax.Precision.HIGHEST, preferred_element_type=F32
+    )
+
+
+def tile_matvec(coupling_ref, own_ref, rows_part, cols_part, pair_sm, rows_ref):
+    tile_rows = coupling_ref.shape[1]
+    first = iota((8, LANES), 1) < HALF
+    which = iota((8, LANES), 0)
+    spread = []
+    for x in range(3):
+        choose = ((first & (which == x)) | (~first & (which == x + 3))).astype(F32)
+        spread.append(exact_dot(rows_part, choose, (((0,), (0,)), ((), ()))))
+    forward = [jnp.zeros((tile_rows, LANES), F32) for _ in range(3)]
+    backward = []
+    for y in range(6):
+        line = cols_part[y : y + 1, :]
+        total = jnp.zeros((8, LANES), F32)
+        for x in range(3):
+            block = coupling_ref[x * 6 + y].astype(F32)
+            forward[x] = forward[x] + block * line
+            weighted = block * spread[x]
+            total = total + jnp.sum(weighted.reshape(tile_rows // 8, 8, LANES), axis=0)
+        line_out = jnp.sum(total, axis=0, keepdims=True)
+        backward.append(line_out + pltpu.roll(line_out, HALF, 1))
+    out = jnp.zeros((8, LANES), F32)
+    for x in range(3):
+        pick = ((first & (which == x)) | (~first & (which == x + 3))).astype(F32)
+        out = out + exact_dot(pick, forward[x], CONTRACT_LAST)
+    rows_ref[...] = rows_part
+    col = lax.axis_index("col")
+    per_col = -(-21 // lax.axis_size("col"))
+    for i in range(per_col):
+        q = jnp.minimum(col * per_col + i, 20)
+        x = pair_sm[q]
+        y = pair_sm[32 + q]
+        weight = own_ref[i : i + 1, :]
+        at_x = rows_ref[pl.ds(x, 1), :] * weight
+        at_y = rows_ref[pl.ds(y, 1), :] * weight
+        out = out + jnp.where(which == x, at_y, 0.0)
+        out = out + jnp.where((which == y) & (x != y), at_x, 0.0)
+    return out, backward
+
+
+def write_partials(out, backward, line, part_ref):
+    first = iota((1, LANES), 1) < HALF
+    rows = [out[x : x + 1, :] for x in range(6)]
+    rows += [jnp.where(first, backward[y], backward[y + 3]) for y in range(3)]
+    if line is not None:
+        rows.append(line)
+    for n in range(part_ref.shape[0]):
+        for k, row in enumerate(rows):
+            part_ref[n, :, k * LANES : (k + 1) * LANES] = row
+
+
+def first_kernel(
+    row_count, col_count, got_ref, map_ref, pair_sm, tile_ref, dense_ref, own_ref, part_ref,
+    wide_ref, rows_ref,
+):
+    devices = got_ref.shape[0]
+    scenes = map_ref.shape[1]
+    scn = scenes // devices
+    per_group = scn // row_count
+    tile_rows = scenes // row_count
+    row = lax.axis_index("row")
+    tiles = jnp.concatenate(
+        [map_ref[:, t * LANES : (t + 1) * LANES] for t in range(scenes // LANES)], axis=0
+    )
+    groups = scenes // LANES
+    place = iota((groups, LANES), 1) % scn
+    rank = jnp.zeros((groups, LANES), jnp.int32)
+    for shift in range(1, scn):
+        before = pltpu.roll(tiles, shift, 1)
+        after = pltpu.roll(tiles, LANES - shift, 1)
+        rank = rank + ((before < tiles) & (place >= shift)).astype(jnp.int32)
+        rank = rank + ((after < tiles) & (place + shift < scn)).astype(jnp.int32)
+    scene_id = iota((groups, LANES), 0) * LANES + iota((groups, LANES), 1)
+    slot_at = (scene_id // scn) * per_group + rank % per_group
+    local = tiles - row * tile_rows
+    slot_at = jnp.where((local >= 0) & (local < tile_rows), slot_at, -1)
+    select = jnp.zeros((tile_rows, tile_rows), F32)
+    for t in range(groups):
+        to_row = jnp.where(iota((tile_rows, LANES), 0) == local[t : t + 1, :], 1.0, 0.0).astype(BF16)
+        from_slot = jnp.where(iota((tile_rows, LANES), 0) == slot_at[t : t + 1, :], 1.0, 0.0).astype(BF16)
+        select = select + lax.dot_general(to_row, from_slot, CONTRACT_LAST, preferred_element_type=F32)
+    select = select.astype(BF16)
+
+    for n in range(devices):
+        wide_ref[pl.ds(n * 96, 96), :] = got_ref[n].astype(F32)
+    for k in range(18):
+        picked = wide_ref[pl.ds(k, tile_rows, stride=24), :].astype(BF16)
+        block = jnp.dot(select, picked, preferred_element_type=F32)
+        dense_ref[k] = block.astype(BF16)
+        tile_ref[k] = block[:, :HALF].astype(BF16)
+        tile_ref[k + 18] = pltpu.roll(block, HALF, 1)[:, :HALF].astype(BF16)
+    extras = []
+    for slot in range(per_group):
+        total = wide_ref[slot * 24 + 16 : slot * 24 + 24, :]
+        for n in range(1, devices):
+            total = total + wide_ref[n * 96 + slot * 24 + 16 : n * 96 + slot * 24 + 24, :]
+        extras.append(pltpu.roll(total, 6, 0))
+    used = iota((8, LANES), 0) < 6
+    rows_part = jnp.where(used, extras[0] + extras[1], 0.0)
+    cols_part = jnp.where(used, extras[2] + pltpu.roll(extras[2], HALF, 1), 0.0)
+    own_ref[...] = extras[3] + pltpu.roll(extras[3], 5, 0)
+    out, backward = tile_matvec(dense_ref, own_ref, rows_part, cols_part, pair_sm, rows_ref)
+    rows_ref[...] = rows_part
+    line = rows_ref[pl.ds(jnp.minimum(lax.axis_index("col"), 5), 1), :]
+    write_partials(out, backward, line, part_ref)
+
+
+def gather_image(row_count, col_count, got_ref, image_ref):
+    first = iota((1, LANES), 1) < HALF
+    side = 6 * LANES
+    cols = []
+    for c in range(col_count):
+        total = got_ref[c, :, side : side + 3 * LANES]
+        for r in range(1, row_count):
+            total = total + got_ref[r * col_count + c, :, side : side + 3 * LANES]
+        cols.append(total)
+    for r in range(row_count):
+        total = got_ref[r * col_count, :, 0:side]
+        for c in range(1, col_count):
+            total = total + got_ref[r * col_count + c, :, 0:side]
+        image_ref[r] = jnp.zeros((8, LANES), F32)
+        for t in range(3):
+            left = cols[2 * r][:, t * LANES : (t + 1) * LANES]
+            right = cols[2 * r + 1][:, t * LANES : (t + 1) * LANES]
+            low = jnp.where(first, left, pltpu.roll(right, HALF, 1))
+            high = jnp.where(first, pltpu.roll(left, HALF, 1), right)
+            image_ref[r, t : t + 1, :] = total[:, t * LANES : (t + 1) * LANES] + low
+            image_ref[r, t + 3 : t + 4, :] = total[:, (t + 3) * LANES : (t + 4) * LANES] + high
+
+
+def inner_all(left, right):
+    return jnp.sum(jnp.sum(left * right, axis=0), keepdims=True)
+
+
+def step_kernel(
+    row_count, col_count, begin, got_ref, dense_ref, own_ref, state_ref, pair_sm, next_ref, part_ref,
+    image_ref, rows_ref,
+):
+    gather_image(row_count, col_count, got_ref, image_ref)
+    if begin:
+        for r in range(row_count):
+            next_ref[1, r] = jnp.zeros((8, LANES), F32)
+            for x in range(6):
+                next_ref[1, r, x : x + 1, :] = got_ref[r * col_count + x, :, 9 * LANES : 10 * LANES]
+        remainder = next_ref[1]
+        direction = remainder
+        answer = jnp.zeros_like(remainder)
+    else:
+        answer, remainder, direction = state_ref[0], state_ref[1], state_ref[2]
+    norm_now = inner_all(remainder, remainder)
+    image = CAMERA_DAMPING * direction + image_ref[...]
+    alpha = norm_now / inner_all(direction, image)
+    answer = answer + alpha * direction
+    remainder = remainder - alpha * image
+    norm_next = inner_all(remainder, remainder)
+    direction = remainder + norm_next / norm_now * direction
+    next_ref[0] = answer
+    next_ref[1] = remainder
+    next_ref[2] = direction
+    col = lax.axis_index("col")
+    rows_part = next_ref[2, lax.axis_index("row")]
+    wide = next_ref[2, lax.div(col, 2)]
+    turned = pltpu.roll(wide, HALF, 1)
+    first = (iota((8, LANES), 1) < HALF).astype(jnp.int32)
+    cols_part = jnp.where(first == 1 - lax.rem(col, 2), wide, turned)
+    out, backward = tile_matvec(dense_ref, own_ref, rows_part, cols_part, pair_sm, rows_ref)
+    write_partials(out, backward, None, part_ref)
+
+
+def last_kernel(row_count, col_count, got_ref, state_ref, answer_ref, remainder_ref, image_ref):
+    gather_image(row_count, col_count, got_ref, image_ref)
+    remainder, direction = state_ref[1], state_ref[2]
+    norm_now = inner_all(remainder, remainder)
+    image_ref[...] = CAMERA_DAMPING * direction + image_ref[...]
+    alpha = norm_now / inner_all(direction, image_ref[...])
+    row = lax.axis_index("row")
+    answer_ref[...] = (state_ref[0, row] + alpha * state_ref[2, row])[:6]
+    remainder_ref[...] = (state_ref[1, row] - alpha * image_ref[row])[:6]
+
+
+def vmem():
+    return pl.BlockSpec(memory_space=pltpu.VMEM)
+
+
+def smem():
+    return pl.BlockSpec(memory_space=pltpu.SMEM)
+
+
+def small_limit(mib):
+    return pltpu.CompilerParams(vmem_limit_bytes=mib << 20)
+
+
+def packed_shards(cam_jac, pt_jac, resid, partner, count, tile_map):
+    row_count = lax.axis_size("row")
+    col_count = lax.axis_size("col")
+    devices = row_count * col_count
+    scenes = tile_map.shape[0]
+    scn, points = partner.shape
+    map_row = tile_map.reshape(1, scenes)
+    pairs = jnp.asarray([p[0] for p in PAIRS] + [0] * 11 + [p[1] for p in PAIRS] + [0] * 11, jnp.int32)
+
+    def bind(kernel, *fixed):
+        def run(*refs):
+            return kernel(row_count, col_count, *fixed, *refs)
+
+        return run
+
+    extra_rows = col_count * 8 + 16
+    send = pl.pallas_call(
+        bind(assemble_kernel),
+        out_shape=jax.ShapeDtypeStruct((devices, 96, LANES), BF16),
+        in_specs=[vmem()] * 5 + [smem()] * 2,
+        out_specs=vmem(),
+        scratch_shapes=[
+            pltpu.VMEM((points // LANES, 64 * scn, LANES), F32),
+            pltpu.VMEM((32 * scn, LANES), F32),
+            pltpu.VMEM((64, scenes), F32),
+            pltpu.VMEM((48 * scn, scenes), BF16),
+            pltpu.VMEM((64, scenes), F32),
+            pltpu.VMEM((extra_rows, scenes), F32),
+            pltpu.VMEM((48 * scn + extra_rows, scenes), F32),
+        ],
+        compiler_params=small_limit(36),
+        name="assemble",
+    )(cam_jac, pt_jac, resid, partner, map_row, count, tile_map)
+    got = lax.all_to_all(send, AXES, 0, 0, tiled=True)
+    tile_rows = scenes // row_count
+    tile, dense, own, part = pl.pallas_call(
+        bind(first_kernel),
+        out_shape=(
+            jax.ShapeDtypeStruct((36, tile_rows, HALF), BF16),
+            jax.ShapeDtypeStruct((18, tile_rows, LANES), BF16),
+            jax.ShapeDtypeStruct((8, LANES), F32),
+            jax.ShapeDtypeStruct((devices, 1, 10 * LANES), F32),
+        ),
+        in_specs=[vmem(), vmem(), smem()],
+        out_specs=(vmem(),) * 4,
+        scratch_shapes=[pltpu.VMEM((devices * 96, LANES), F32), pltpu.VMEM((8, LANES), F32)],
+        compiler_params=small_limit(16),
+        name="first",
+    )(got, map_row, pairs)
+    state = jnp.zeros((3, row_count, 8, LANES), F32)
+    for turn in range(ITERS - 1):
+        got = lax.all_to_all(part, AXES, 0, 0, tiled=True)
+        state, part = pl.pallas_call(
+            bind(step_kernel, turn == 0),
+            out_shape=(
+                jax.ShapeDtypeStruct((3, row_count, 8, LANES), F32),
+                jax.ShapeDtypeStruct((devices, 1, 9 * LANES), F32),
+            ),
+            in_specs=[vmem()] * 4 + [smem()],
+            out_specs=(vmem(),) * 2,
+            scratch_shapes=[pltpu.VMEM((row_count, 8, LANES), F32), pltpu.VMEM((8, LANES), F32)],
+            compiler_params=small_limit(8),
+            name="step",
+        )(got, dense, own, state, pairs)
+    got = lax.all_to_all(part, AXES, 0, 0, tiled=True)
+    answer, remainder = pl.pallas_call(
+        bind(last_kernel),
+        out_shape=(jax.ShapeDtypeStruct((6, tile_rows), F32),) * 2,
+        in_specs=[vmem()] * 2,
+        out_specs=(vmem(),) * 2,
+        scratch_shapes=[pltpu.VMEM((row_count, 8, LANES), F32)],
+        compiler_params=small_limit(4),
+        name="last",
+    )(got, state)
+    return tile.reshape(6, 6, tile_rows, HALF), answer, remainder
 
 
 def cross_product(first_vec, second_vec):
@@ -79,7 +587,7 @@
     return (solution, remainder)
 
 
-def shards(cam_jac, pt_jac, resid, partner, count, tile_map):
+def plain_shards(cam_jac, pt_jac, resid, partner, count, tile_map):
     row_count = lax.axis_size("row")
     col_count = lax.axis_size("col")
     scenes = tile_map.shape[0]
@@ -201,16 +709,33 @@
     return (coupling_tile, solution, remainder)
 
 
+def shards(cam_jac, pt_jac, resid, partner, count, tile_map):
+    row_count = lax.axis_size("row")
+    col_count = lax.axis_size("col")
+    scenes = tile_map.shape[0]
+    scn, points = partner.shape
+    packs = (
+        scenes == col_count * HALF
+        and scenes == row_count * LANES
+        and scn == row_count * 4
+        and LANES % scn == 0
+        and points % LANES == 0
+        and col_count >= 7
+    )
+    run = packed_shards if packs else plain_shards
+    return run(cam_jac, pt_jac, resid, partner, count, tile_map)
+
+
 def solution(mesh):
     return jax.shard_map(
         shards,
         mesh=mesh,
         in_specs=(
-            P(None, None, None, ("row", "col"), None),
-            P(None, None, None, ("row", "col"), None),
-            P(None, None, ("row", "col"), None),
-            P(("row", "col"), None),
-            P(("row", "col")),
+            P(None, None, None, AXES, None),
+            P(None, None, None, AXES, None),
+            P(None, None, AXES, None),
+            P(AXES, None),
+            P(AXES),
             P(),
         ),
         out_specs=(P(None, None, "row", "col"), P(None, "row"), P(None, "row")),

time: 398 us -> 84.8 us (0.21)
  blocking collectives: 162 us -> 50 us
  waiting for transfers between devices: 71.8 us -> 7.09 us
  local copies, waits for them, and re-layouts: 53.9 us -> 6.48 us
  other arithmetic: 44.9 us -> 0 us
  matrix products: 33.6 us -> 0 us
  between operations: 21.2 us -> 0.69 us
  Pallas kernels: 0 us -> 17.6 us
  starting transfers between devices: 7.36 us -> 2.57 us
    psum x4 -> x0, blocking collectives: 162 us -> none  [the longest x3 121 us: tile_products(): return lax.psum(spread, ('row', 'col'))]
    psum x1 -> x0, waiting for transfers between devices: 71.8 us -> none  [shards(): diag_all, grad_all = lax.psum((diag_part, grad_part), ('row', 'col'))]
    all_to_all x0 -> x3, blocking collectives: none -> 50 us  [the longest x1 29 us: packed_shards(): got = lax.all_to_all(send, AXES, 0, 0, tiled=True)]
    dynamic_slice x39 -> x0, local copies, waits for them, and re-layouts: 44.8 us -> none  [the longest x32 44.5 us: shards(): per_scene = lax.map(scene_sums, (values, partner))]
    dot_general x25 -> x0, matrix products: 33.6 us -> none  [the longest x16 26.2 us: scene_sums(): jnp.dot(scene_values, onehot, precision=lax.Precision.HIGHEST, preferred_...]
    reduce_sum x35 -> x0, other arithmetic: 28.8 us -> none  [the longest x16 7.48 us: scene_sums(): tile_other = jnp.sum(jnp.where(hits, tile_map[None, :], 0), axis=1)]
    pallas_call x0 -> x5, Pallas kernels: none -> 17.6 us  [the longest x1 10.9 us: packed_shards(): pl.pallas_call(bind(assemble_kernel), out_shape=jax.ShapeDtypeStruct((dev...]
    all_to_all x1, waiting for transfers between devices: 0.01 us -> 7.09 us  [packed_shards(): got = lax.all_to_all(part, AXES, 0, 0, tiled=True)]
  transfers between devices with their start and end apart: 2 -> 1, of which waited for: 1 -> 1; matrix products, arithmetic and copies ran while one was open for 2% -> 2% of each run, Pallas kernels for 0% -> 0%
where the time goes in v1:
time: 84.8 us; the launch traced here: 84.4 us
  blocking collectives  50 us (59%)
  Pallas kernels  17.6 us (21%)
  waiting for transfers between devices  7.09 us (8%)
  local copies, waits for them, and re-layouts  6.48 us (8%)
  starting transfers between devices  2.57 us (3%)
    all_to_all x1, blocking collectives, packed_shards(): got = lax.all_to_all(send, AXES, 0, 0, tiled=True)  29 us
    all_to_all x2, blocking collectives, packed_shards(): got = lax.all_to_all(part, AXES, 0, 0, tiled=True)  21 us
    pallas_call x1, Pallas kernels, packed_shards(): pl.pallas_call(bind(assemble_kernel), out_shape=jax.ShapeDtypeStruct((dev...  10.9 us
    all_to_all x1, waiting for transfers between devices, packed_shards(): got = lax.all_to_all(part, AXES, 0, 0, tiled=True)  7.09 us
    unnamed x15, local copies, waits for them, and re-layouts  6.48 us
    pallas_call x2, Pallas kernels, packed_shards(): pl.pallas_call(bind(step_kernel, turn == 0), out_shape=(jax.ShapeDtypeStr...  3.95 us
    all_to_all x1, starting transfers between devices, packed_shards(): got = lax.all_to_all(part, AXES, 0, 0, tiled=True)  2.57 us
    pallas_call x1, Pallas kernels, packed_shards(): pl.pallas_call(bind(first_kernel), out_shape=(jax.ShapeDtypeStruct((36, t...  1.98 us
  transfers between devices with their start and end apart: 1, of which 1 were waited for; matrix products, arithmetic and copies ran while one was open for 2% of the time, Pallas kernels for 0%

profile of v1, /device:TPU:0, one launch (start us, length us, event | category | flops | bytes accessed | tf_op | source)
XLA Modules:
  0.0 84.4 jit_solution(1954796337956724298)
XLA Ops:
  0.6 0.0 copy-start
  0.6 1.1 %copy-done = bf16[2,2,6,16,1024]{4,3,2,1,0:T(8,128)(2,1)S(1)} copy-done((bf16[2,2,6,16,1024]{4,3,2,1,0:T(8,128)(2,1)S(1)}, bf16[2,2,6,16,1024]{4,3,2,1,0:T(8,128)(2,1)}, u32[]{:S(2)}) %copy-start) | copy-done | bytes 786456
  1.8 0.0 copy-start.1
  1.8 1.0 %copy-done.1 = bf16[2,2,3,16,1024]{4,3,2,1,0:T(8,128)(2,1)S(1)} copy-done((bf16[2,2,3,16,1024]{4,3,2,1,0:T(8,128)(2,1)S(1)}, bf16[2,2,3,16,1024]{4,3,2,1,0:T(8,128)(2,1)}, u32[]{:S(2)}) %copy-start.1) | copy-done | bytes 393240
  2.8 0.0 copy-start.2
  2.8 0.9 %copy-done.2 = bf16[2,2,16,1024]{3,2,1,0:T(8,128)(2,1)S(1)} copy-done((bf16[2,2,16,1024]{3,2,1,0:T(8,128)(2,1)S(1)}, bf16[2,2,16,1024]{3,2,1,0:T(8,128)(2,1)}, u32[]{:S(2)}) %copy-start.2) | copy-done | bytes 131096
  3.7 0.0 copy-start.3
  3.7 0.8 copy-done.3
  4.5 0.0 copy-start.4
  4.5 0.7 copy-done.4
  5.2 0.7 copy-done.6
  5.8 10.9 %assemble.1 = bf16[32,96,128]{2,1,0:T(8,128)(2,1)S(1)} custom-call(bf16[2,2,6,16,1024]{4,3,2,1,0:T(8,128)(2,1)S(1)} %copy-done, bf16[2,2,3,16,1024]{4,3,2,1,0:T(8,128)(2,1)S(1)} %copy-done.1, bf16[2,2,16,1024]{3,2,1,0:T(8,128)(2,1)S(1)} %copy-done.2, s32[16,1024]{1,0:T(8,128)S(1)} %copy-done.3, s32[1,512]{1,0:T(1,128)S(1)} %bitcast.3, s32[16]{0:T(128)S(1)} %copy-done.6, ...), custom_call_target="tpu_custom_call" | custom-call | tf_op jit(solution)/shard_map/assemble/pallas_call | solution.py:460
  16.7 0.0 copy-start.5
  16.7 29.0 %all_to_all.20.refs_0_ = bf16[32,96,128]{2,1,0:T(8,128)(2,1)S(1)} all-to-all(bf16[32,96,128]{2,1,0:T(8,128)(2,1)S(1)} %assemble.1), channel_id=1, replica_groups=mesh['row'=4,'col'=8] {'row','col'}, dimensions={0} | all-to-all | bytes 1572864 | tf_op jit(solution)/shard_map/all_to_all | solution.py:477
  45.7 0.0 copy-done.5
  45.7 2.0 %first.1 = (bf16[36,128,64]{2,1,0:T(8,128)(2,1)S(1)}, bf16[18,128,128]{2,1,0:T(8,128)(2,1)S(1)}, f32[8,128]{1,0:T(8,128)S(1)}, f32[32,1,1280]{2,1,0:T(1,128)S(1)}) custom-call(bf16[32,96,128]{2,1,0:T(8,128)(2,1)S(1)} %all_to_all.20.refs_0_, s32[1,512]{1,0:T(1,128)S(1)} %bitcast.4, s32[64]{0:T(128)S(1)} %copy-done.5), custom_call_target="tpu_custom_call" | custom-call | tf_op jit(solution)/shard_map/first/pallas_call | solution.py:479
  47.7 10.6 %all_to_all.21.refs_0_ = f32[32,1,1280]{2,1,0:T(1,128)S(1)} all-to-all(f32[32,1,1280]{2,1,0:T(1,128)S(1)} %get-tuple-element.14), channel_id=1, replica_groups=mesh['row'=4,'col'=8] {'row','col'}, dimensions={0} | all-to-all | bytes 327680 | tf_op jit(solution)/shard_map/all_to_all | solution.py:495
  58.3 1.6 %step.2 = (f32[3,4,8,128]{3,2,1,0:T(8,128)S(1)}, f32[32,1,1152]{2,1,0:T(1,128)S(1)}) custom-call(f32[32,1,1280]{2,1,0:T(1,128)S(1)} %all_to_all.21.refs_0_, bf16[18,128,128]{2,1,0:T(8,128)(2,1)S(1)} %get-tuple-element.15.refs_1_, f32[8,128]{1,0:T(8,128)S(1)} %get-tuple-element.16.refs_2_, f32[3,4,8,128]{3,2,1,0:T(8,128)S(1)} %broadcast_in_dim.3.refs_3_, ...), custom_call_target="tpu_custom_call" | custom-call | tf_op jit(solution)/shard_map/step/pallas_call | solution.py:496
  60.0 10.4 %all_to_all.22.refs_0_ = f32[32,1,1152]{2,1,0:T(1,128)S(1)} all-to-all(f32[32,1,1152]{2,1,0:T(1,128)S(1)} %get-tuple-element.17), channel_id=1, replica_groups=mesh['row'=4,'col'=8] {'row','col'}, dimensions={0} | all-to-all | bytes 294912 | tf_op jit(solution)/shard_map/all_to_all | solution.py:495
  70.3 2.3 %step.3 = (f32[3,4,8,128]{3,2,1,0:T(8,128)S(1)}, f32[32,1,1152]{2,1,0:T(1,128)}) custom-call(f32[32,1,1152]{2,1,0:T(1,128)S(1)} %all_to_all.22.refs_0_, bf16[18,128,128]{2,1,0:T(8,128)(2,1)S(1)} %get-tuple-element.15.refs_1_, f32[8,128]{1,0:T(8,128)S(1)} %get-tuple-element.16.refs_2_, f32[3,4,8,128]{3,2,1,0:T(8,128)S(1)} %get-tuple-element.18.refs_3_, ...), custom_call_target="tpu_custom_call" | custom-call | tf_op jit(solution)/shard_map/step/pallas_call | solution.py:496
  72.7 2.6 %all-to-all-start.3 = ((f32[32,1,1152]{2,1,0:T(1,128)}), f32[32,1,1152]{2,1,0:T(1,128)S(1)}, u32[]{:S(2)}, u32[]{:S(2)}) async-start(f32[32,1,1152]{2,1,0:T(1,128)} %get-tuple-element.19), calls=%async_computation.3 | async-start | bytes 294912 | tf_op jit(solution)/shard_map/all_to_all | solution.py:508
  75.2 1.3 %copy.10 = bf16[6,6,128,64]{2,3,1,0:T(8,128)(2,1)} copy(bf16[6,6,128,64]{3,2,1,0:T(8,128)(2,1)S(1)} %bitcast.2) | data formatting | bytes 1179648
  76.5 7.1 %all-to-all-done.3.refs_0_ = f32[32,1,1152]{2,1,0:T(1,128)S(1)} async-done(((f32[32,1,1152]{2,1,0:T(1,128)}), f32[32,1,1152]{2,1,0:T(1,128)S(1)}, u32[]{:S(2)}, u32[]{:S(2)}) %all-to-all-start.3) | async-done | bytes 147488 | tf_op jit(solution)/shard_map/all_to_all | solution.py:508
  83.6 0.8 last.1
  (2 shorter events, 0.0 us)
Async XLA Ops:
  0.6 1.1 %copy-start = (bf16[2,2,6,16,1024]{4,3,2,1,0:T(8,128)(2,1)S(1)}, bf16[2,2,6,16,1024]{4,3,2,1,0:T(8,128)(2,1)}, u32[]{:S(2)}) copy-start(bf16[2,2,6,16,1024]{4,3,2,1,0:T(8,128)(2,1)} %refs_0_.1) | copy-start | bytes 2359300
  1.8 1.0 %copy-start.1 = (bf16[2,2,3,16,1024]{4,3,2,1,0:T(8,128)(2,1)S(1)}, bf16[2,2,3,16,1024]{4,3,2,1,0:T(8,128)(2,1)}, u32[]{:S(2)}) copy-start(bf16[2,2,3,16,1024]{4,3,2,1,0:T(8,128)(2,1)} %refs_1_.1) | copy-start | bytes 1179652
  2.8 0.9 %copy-start.2 = (bf16[2,2,16,1024]{3,2,1,0:T(8,128)(2,1)S(1)}, bf16[2,2,16,1024]{3,2,1,0:T(8,128)(2,1)}, u32[]{:S(2)}) copy-start(bf16[2,2,16,1024]{3,2,1,0:T(8,128)(2,1)} %refs_2_.2) | copy-start | bytes 393220
  3.7 0.8 copy-start.3
  4.5 0.7 copy-start.4
  5.2 0.7 copy-start.6
  16.7 29.0 %copy-start.5 = (s32[64]{0:T(128)S(1)}, s32[64]{0:T(128)}, u32[]{:S(2)}) copy-start(s32[64]{0:T(128)} %constant.4.clone.refs_2_.refs_4_) | copy-start | bytes 772
  72.7 10.9 %all-to-all-start.3 = ((f32[32,1,1152]{2,1,0:T(1,128)}), f32[32,1,1152]{2,1,0:T(1,128)S(1)}, u32[]{:S(2)}, u32[]{:S(2)}) async-start(f32[32,1,1152]{2,1,0:T(1,128)} %get-tuple-element.19), calls=%async_computation.3 | async-start | bytes 294912 | tf_op jit(solution)/shard_map/all_to_all | solution.py:508

commit v2 on v1

--- a/solution.py
+++ b/solution.py
@@ -25,12 +25,6 @@
     high = value.astype(BF16)
     low = (value - high.astype(F32)).astype(BF16)
     return high, low
-
-
-def dot2(left, right):
-    a, b = left
-    c, d = right
-    return a * c + b * d
 
 
 def point_values(ja, jb, pa, pb, ea, eb, live):
@@ -100,25 +94,53 @@
 
 
 def assemble_kernel(
-    row_count, col_count, cam_ref, pt_ref, res_ref, partner_ref, map_ref, count_sm, map_sm, send_ref,
+    row_count, col_count, cam_in, pt_in, res_in, partner_in, row_in, count_in, map_in, send_ref,
     vals_ref, own_ref, acc_ref, links_ref, flat_ref, extra_ref, perm_ref,
+    cam_ref, pt_ref, res_ref, partner_ref, map_ref, count_sm, map_sm, slab_sem, whole_sem,
 ):
     scn = partner_ref.shape[0]
     points = partner_ref.shape[1]
     scenes = map_ref.shape[1]
+    wholes = [
+        pltpu.make_async_copy(source, target, whole_sem.at[k])
+        for k, (source, target) in enumerate(
+            [(count_in, count_sm), (map_in, map_sm), (row_in, map_ref), (partner_in, partner_ref)]
+        )
+    ]
+
+    def slab_copies(step):
+        lanes = pl.ds(pl.multiple_of(step * LANES, LANES), LANES)
+        return [
+            pltpu.make_async_copy(
+                source.at[..., lanes], target.at[..., lanes], slab_sem.at[k, step]
+            )
+            for k, (source, target) in enumerate([(cam_in, cam_ref), (pt_in, pt_ref), (res_in, res_ref)])
+        ]
+
+    wholes[0].start()
+    for step in range(points // LANES):
+        for copy in slab_copies(step):
+            copy.start()
+    for copy in wholes[1:]:
+        copy.start()
     per_group = scn // row_count
     device = lax.axis_index("row") * col_count + lax.axis_index("col")
     slab = (scn, LANES)
 
+    own_ref[...] = jnp.zeros_like(own_ref)
+    acc_ref[...] = jnp.zeros_like(acc_ref)
+    extra_ref[...] = jnp.zeros_like(extra_ref)
+    vals_ref[:, pl.ds(63 * scn, scn), :] = jnp.zeros((points // LANES, scn, LANES), F32)
+
+    wholes[0].wait()
     sub = iota(slab, 0)
     counts = jnp.zeros(slab, jnp.int32)
     for s in range(scn):
         counts = jnp.where(sub == s, count_sm[s], counts)
-    own_ref[...] = jnp.zeros_like(own_ref)
-    acc_ref[...] = jnp.zeros_like(acc_ref)
-    vals_ref[:, pl.ds(63 * scn, scn), :] = jnp.zeros((points // LANES, scn, LANES), F32)
 
     def slab_step(step, carry):
+        for copy in slab_copies(step):
+            copy.wait()
         lanes = pl.ds(pl.multiple_of(step * LANES, LANES), LANES)
 
         def get(ref, *where):
@@ -153,6 +175,8 @@
 
     lax.fori_loop(0, points // LANES, slab_step, 0)
 
+    for copy in wholes[1:]:
+        copy.wait()
     spots = iota((scenes, points), 0)
 
     def scene_step(s, carry):
@@ -172,7 +196,7 @@
         links_ref[pl.ds(pl.multiple_of(rank * 48, 16), 48), :] = total[:48].astype(BF16)
         return carry
 
-    lax.fori_loop(0, scn, scene_step, 0)
+    lax.fori_loop(0, scn, scene_step, 0, unroll=4)
 
     lane = iota((32, LANES), 1)
     own = jnp.zeros((32, LANES), F32)
@@ -190,7 +214,6 @@
         flat_ref[0:32, cols] = high.astype(F32)
         flat_ref[32:64, cols] = low.astype(F32)
     per_col = -(-21 // col_count)
-    extra_ref[...] = jnp.zeros_like(extra_ref)
     for c in range(col_count):
         for i in range(per_col):
             q = c * per_col + i
@@ -244,36 +267,26 @@
                     send_ref[r * col_count + c, slot * 24 : slot * 24 + 24, :] = block.astype(BF16)
 
 
-def exact_dot(left, right, dims):
-    return lax.dot_general(
-        left, right, dims, precision=lax.Precision.HIGHEST, preferred_element_type=F32
-    )
-
-
-def tile_matvec(coupling_ref, own_ref, rows_part, cols_part, pair_sm, rows_ref):
-    tile_rows = coupling_ref.shape[1]
-    first = iota((8, LANES), 1) < HALF
+def tile_matvec(tile_ref, own_ref, rows_part, cols_part, pair_sm, rows_ref):
     which = iota((8, LANES), 0)
-    spread = []
-    for x in range(3):
-        choose = ((first & (which == x)) | (~first & (which == x + 3))).astype(F32)
-        spread.append(exact_dot(rows_part, choose, (((0,), (0,)), ((), ()))))
-    forward = [jnp.zeros((tile_rows, LANES), F32) for _ in range(3)]
+    turned = jnp.transpose(cols_part)[:HALF]
+    forward = [jnp.zeros((8, LANES), F32) for _ in range(6)]
     backward = []
     for y in range(6):
-        line = cols_part[y : y + 1, :]
-        total = jnp.zeros((8, LANES), F32)
-        for x in range(3):
-            block = coupling_ref[x * 6 + y].astype(F32)
-            forward[x] = forward[x] + block * line
-            weighted = block * spread[x]
-            total = total + jnp.sum(weighted.reshape(tile_rows // 8, 8, LANES), axis=0)
-        line_out = jnp.sum(total, axis=0, keepdims=True)
-        backward.append(line_out + pltpu.roll(line_out, HALF, 1))
+        column = jnp.broadcast_to(turned[:, y : y + 1], (HALF, LANES))
+        total = jnp.zeros((HALF, LANES), F32)
+        for x in range(6):
+            block = tile_ref[x * 6 + y].astype(F32)
+            forward[x] = forward[x] + jnp.sum((block * column).reshape(HALF // 8, 8, LANES), axis=0)
+            total = total + block * rows_part[x : x + 1, :]
+        backward.append(total)
+    sides = []
+    for y in range(3):
+        pair = jnp.concatenate([backward[y], backward[y + 3]], axis=0)
+        sides.append(jnp.sum(jnp.transpose(pair), axis=0, keepdims=True))
     out = jnp.zeros((8, LANES), F32)
-    for x in range(3):
-        pick = ((first & (which == x)) | (~first & (which == x + 3))).astype(F32)
-        out = out + exact_dot(pick, forward[x], CONTRACT_LAST)
+    for x in range(6):
+        out = jnp.where(which == x, jnp.sum(forward[x], axis=0, keepdims=True), out)
     rows_ref[...] = rows_part
     col = lax.axis_index("col")
     per_col = -(-21 // lax.axis_size("col"))
@@ -286,13 +299,11 @@
         at_y = rows_ref[pl.ds(y, 1), :] * weight
         out = out + jnp.where(which == x, at_y, 0.0)
         out = out + jnp.where((which == y) & (x != y), at_x, 0.0)
-    return out, backward
-
-
-def write_partials(out, backward, line, part_ref):
-    first = iota((1, LANES), 1) < HALF
-    rows = [out[x : x + 1, :] for x in range(6)]
-    rows += [jnp.where(first, backward[y], backward[y + 3]) for y in range(3)]
+    return out, sides
+
+
+def write_partials(out, sides, line, part_ref):
+    rows = [out[x : x + 1, :] for x in range(6)] + sides
     if line is not None:
         rows.append(line)
     for n in range(part_ref.shape[0]):
@@ -301,8 +312,7 @@
 
 
 def first_kernel(
-    row_count, col_count, got_ref, map_ref, pair_sm, tile_ref, dense_ref, own_ref, part_ref,
-    wide_ref, rows_ref,
+    row_count, col_count, got_ref, map_ref, pair_sm, tile_ref, own_ref, part_ref, wide_ref, rows_ref,
 ):
     devices = got_ref.shape[0]
     scenes = map_ref.shape[1]
@@ -336,10 +346,9 @@
         wide_ref[pl.ds(n * 96, 96), :] = got_ref[n].astype(F32)
     for k in range(18):
         picked = wide_ref[pl.ds(k, tile_rows, stride=24), :].astype(BF16)
-        block = jnp.dot(select, picked, preferred_element_type=F32)
-        dense_ref[k] = block.astype(BF16)
-        tile_ref[k] = block[:, :HALF].astype(BF16)
-        tile_ref[k + 18] = pltpu.roll(block, HALF, 1)[:, :HALF].astype(BF16)
+        block = lax.dot_general(picked, select, (((0,), (1,)), ((), ())), preferred_element_type=F32)
+        tile_ref[k] = block[:HALF].astype(BF16)
+        tile_ref[k + 18] = block[HALF:].astype(BF16)
     extras = []
     for slot in range(per_group):
         total = wide_ref[slot * 24 + 16 : slot * 24 + 24, :]
@@ -350,10 +359,10 @@
     rows_part = jnp.where(used, extras[0] + extras[1], 0.0)
     cols_part = jnp.where(used, extras[2] + pltpu.roll(extras[2], HALF, 1), 0.0)
     own_ref[...] = extras[3] + pltpu.roll(extras[3], 5, 0)
-    out, backward = tile_matvec(dense_ref, own_ref, rows_part, cols_part, pair_sm, rows_ref)
+    out, sides = tile_matvec(tile_ref, own_ref, rows_part, cols_part, pair_sm, rows_ref)
     rows_ref[...] = rows_part
     line = rows_ref[pl.ds(jnp.minimum(lax.axis_index("col"), 5), 1), :]
-    write_partials(out, backward, line, part_ref)
+    write_partials(out, sides, line, part_ref)
 
 
 def gather_image(row_count, col_count, got_ref, image_ref):
@@ -384,9 +393,15 @@
 
 
 def step_kernel(
-    row_count, col_count, begin, got_ref, dense_ref, own_ref, state_ref, pair_sm, next_ref, part_ref,
-    image_ref, rows_ref,
+    row_count, col_count, begin, got_ref, tile_ref, own_ref, state_ref, pair_sm, next_ref, part_ref,
+    *rest,
 ):
+    if begin:
+        coupling_ref, image_ref, rows_ref, copy_sem = rest
+        copy = pltpu.make_async_copy(tile_ref, coupling_ref, copy_sem)
+        copy.start()
+    else:
+        image_ref, rows_ref = rest
     gather_image(row_count, col_count, got_ref, image_ref)
     if begin:
         for r in range(row_count):
@@ -412,10 +427,11 @@
     rows_part = next_ref[2, lax.axis_index("row")]
     wide = next_ref[2, lax.div(col, 2)]
     turned = pltpu.roll(wide, HALF, 1)
-    first = (iota((8, LANES), 1) < HALF).astype(jnp.int32)
-    cols_part = jnp.where(first == 1 - lax.rem(col, 2), wide, turned)
-    out, backward = tile_matvec(dense_ref, own_ref, rows_part, cols_part, pair_sm, rows_ref)
-    write_partials(out, backward, None, part_ref)
+    cols_part = jnp.where(iota((8, LANES), 0) * 0 == lax.rem(col, 2), wide, turned)
+    out, sides = tile_matvec(tile_ref, own_ref, rows_part, cols_part, pair_sm, rows_ref)
+    write_partials(out, sides, None, part_ref)
+    if begin:
+        copy.wait()
 
 
 def last_kernel(row_count, col_count, got_ref, state_ref, answer_ref, remainder_ref, image_ref):
@@ -437,6 +453,10 @@
     return pl.BlockSpec(memory_space=pltpu.SMEM)
 
 
+def hbm():
+    return pl.BlockSpec(memory_space=pltpu.HBM)
+
+
 def small_limit(mib):
     return pltpu.CompilerParams(vmem_limit_bytes=mib << 20)
 
@@ -460,7 +480,7 @@
     send = pl.pallas_call(
         bind(assemble_kernel),
         out_shape=jax.ShapeDtypeStruct((devices, 96, LANES), BF16),
-        in_specs=[vmem()] * 5 + [smem()] * 2,
+        in_specs=[hbm()] * 7,
         out_specs=vmem(),
         scratch_shapes=[
             pltpu.VMEM((points // LANES, 64 * scn, LANES), F32),
@@ -470,22 +490,30 @@
             pltpu.VMEM((64, scenes), F32),
             pltpu.VMEM((extra_rows, scenes), F32),
             pltpu.VMEM((48 * scn + extra_rows, scenes), F32),
+            pltpu.VMEM(cam_jac.shape, BF16),
+            pltpu.VMEM(pt_jac.shape, BF16),
+            pltpu.VMEM(resid.shape, BF16),
+            pltpu.VMEM(partner.shape, jnp.int32),
+            pltpu.VMEM(map_row.shape, jnp.int32),
+            pltpu.SMEM(count.shape, jnp.int32),
+            pltpu.SMEM(tile_map.shape, jnp.int32),
+            pltpu.SemaphoreType.DMA((3, points // LANES)),
+            pltpu.SemaphoreType.DMA((4,)),
         ],
         compiler_params=small_limit(36),
         name="assemble",
-    )(cam_jac, pt_jac, resid, partner, map_row, count, tile_map)
+    )(*[pltpu.with_memory_space_constraint(v, pltpu.HBM) for v in (cam_jac, pt_jac, resid, partner, map_row, count, tile_map)])
     got = lax.all_to_all(send, AXES, 0, 0, tiled=True)
     tile_rows = scenes // row_count
-    tile, dense, own, part = pl.pallas_call(
+    tile, own, part = pl.pallas_call(
         bind(first_kernel),
         out_shape=(
-            jax.ShapeDtypeStruct((36, tile_rows, HALF), BF16),
-            jax.ShapeDtypeStruct((18, tile_rows, LANES), BF16),
+            jax.ShapeDtypeStruct((36, HALF, tile_rows), BF16),
             jax.ShapeDtypeStruct((8, LANES), F32),
             jax.ShapeDtypeStruct((devices, 1, 10 * LANES), F32),
         ),
         in_specs=[vmem(), vmem(), smem()],
-        out_specs=(vmem(),) * 4,
+        out_specs=(vmem(),) * 3,
         scratch_shapes=[pltpu.VMEM((devices * 96, LANES), F32), pltpu.VMEM((8, LANES), F32)],
         compiler_params=small_limit(16),
         name="first",
@@ -493,18 +521,28 @@
     state = jnp.zeros((3, row_count, 8, LANES), F32)
     for turn in range(ITERS - 1):
         got = lax.all_to_all(part, AXES, 0, 0, tiled=True)
-        state, part = pl.pallas_call(
-            bind(step_kernel, turn == 0),
-            out_shape=(
-                jax.ShapeDtypeStruct((3, row_count, 8, LANES), F32),
-                jax.ShapeDtypeStruct((devices, 1, 9 * LANES), F32),
-            ),
+        begin = turn == 0
+        outs = [
+            jax.ShapeDtypeStruct((3, row_count, 8, LANES), F32),
+            jax.ShapeDtypeStruct((devices, 1, 9 * LANES), F32),
+        ]
+        places = [vmem()] * 2
+        scratch = [pltpu.VMEM((row_count, 8, LANES), F32), pltpu.VMEM((8, LANES), F32)]
+        if begin:
+            outs.append(jax.ShapeDtypeStruct(tile.shape, BF16))
+            places.append(hbm())
+            scratch.append(pltpu.SemaphoreType.DMA(()))
+        state, part, *rest = pl.pallas_call(
+            bind(step_kernel, begin),
+            out_shape=outs,
             in_specs=[vmem()] * 4 + [smem()],
-            out_specs=(vmem(),) * 2,
-            scratch_shapes=[pltpu.VMEM((row_count, 8, LANES), F32), pltpu.VMEM((8, LANES), F32)],
+            out_specs=places,
+            scratch_shapes=scratch,
             compiler_params=small_limit(8),
             name="step",
-        )(got, dense, own, state, pairs)
+        )(got, tile, own, state, pairs)
+        if begin:
+            coupling = rest[0]
     got = lax.all_to_all(part, AXES, 0, 0, tiled=True)
     answer, remainder = pl.pallas_call(
         bind(last_kernel),
@@ -515,7 +553,7 @@
         compiler_params=small_limit(4),
         name="last",
     )(got, state)
-    return tile.reshape(6, 6, tile_rows, HALF), answer, remainder
+    return jnp.swapaxes(coupling.reshape(6, 6, HALF, tile_rows), 2, 3), answer, remainder
 
 
 def cross_product(first_vec, second_vec):

time: 84.8 us -> 76.1 us (0.90)
  blocking collectives: 50 us -> 60.2 us
  waiting for transfers between devices: 7.09 us -> 0 us
  local copies, waits for them, and re-layouts: 6.48 us -> 0.02 us
  Pallas kernels: 17.6 us -> 15 us
  starting transfers between devices: 2.57 us -> 0 us
    all_to_all x2 -> x3, blocking collectives: 21 us -> 31.2 us  [packed_shards(): got = lax.all_to_all(part, AXES, 0, 0, tiled=True)]
    all_to_all x1 -> x0, waiting for transfers between devices: 7.09 us -> none  [packed_shards(): got = lax.all_to_all(part, AXES, 0, 0, tiled=True)]
    unnamed x15 -> x4, local copies, waits for them, and re-layouts: 6.48 us -> 0.01 us
    all_to_all x1 -> x0, starting transfers between devices: 2.57 us -> none  [packed_shards(): got = lax.all_to_all(part, AXES, 0, 0, tiled=True)]
    pallas_call x3, Pallas kernels: 5.93 us -> 4.41 us  [the longest x2 2.72 us: packed_shards(): pl.pallas_call(bind(step_kernel, begin), out_shape=outs, in_specs=[vmem()...]
    pallas_call x1, Pallas kernels: 10.9 us -> 9.75 us  [packed_shards(): pl.pallas_call(bind(assemble_kernel), out_shape=jax.ShapeDtypeStruct((dev...]
  transfers between devices with their start and end apart: 1 -> 0, of which waited for: 1 -> 0; matrix products, arithmetic and copies ran while one was open for 2% -> 0% of each run, Pallas kernels for 0% -> 0%
where the time goes in v2:
time: 76.1 us; the launch traced here: 75.9 us
  blocking collectives  60.2 us (79%)
  Pallas kernels  15 us (20%)
    all_to_all x3, blocking collectives, packed_shards(): got = lax.all_to_all(part, AXES, 0, 0, tiled=True)  31.2 us
    all_to_all x1, blocking collectives, packed_shards(): got = lax.all_to_all(send, AXES, 0, 0, tiled=True)  29 us
    pallas_call x1, Pallas kernels, packed_shards(): pl.pallas_call(bind(assemble_kernel), out_shape=jax.ShapeDtypeStruct((dev...  9.75 us
    pallas_call x2, Pallas kernels, packed_shards(): pl.pallas_call(bind(step_kernel, begin), out_shape=outs, in_specs=[vmem()...  2.72 us
    pallas_call x1, Pallas kernels, packed_shards(): pl.pallas_call(bind(first_kernel), out_shape=(jax.ShapeDtypeStruct((36, H...  1.69 us

profile of v2, /device:TPU:0, one launch (start us, length us, event | category | flops | bytes accessed | tf_op | source)
XLA Modules:
  0.0 75.9 jit_solution(10991406790560197966)
XLA Ops:
  0.6 9.8 %assemble.1 = bf16[32,96,128]{2,1,0:T(8,128)(2,1)S(1)} custom-call(bf16[2,2,6,16,1024]{4,3,2,1,0:T(8,128)(2,1)} %refs_0_.1, bf16[2,2,3,16,1024]{4,3,2,1,0:T(8,128)(2,1)} %refs_1_.1, bf16[2,2,16,1024]{3,2,1,0:T(8,128)(2,1)} %refs_2_.2, s32[16,1024]{1,0:T(8,128)} %refs_3_.1, s32[1,512]{1,0:T(1,128)} %bitcast.4, s32[16]{0:T(128)} %refs_5_.1, s32[512]{0:T(512)} %refs_6_.1), custom_call_target="tpu_custom_call" | custom-call | tf_op jit(solution)/shard_map/assemble/pallas_call | solution.py:480
  10.4 0.0 copy-start
  10.4 0.0 copy-start.1
  10.4 29.0 %all_to_all.20.refs_0_ = bf16[32,96,128]{2,1,0:T(8,128)(2,1)S(1)} all-to-all(bf16[32,96,128]{2,1,0:T(8,128)(2,1)S(1)} %assemble.1), channel_id=1, replica_groups=mesh['row'=4,'col'=8] {'row','col'}, dimensions={0} | all-to-all | bytes 1572864 | tf_op jit(solution)/shard_map/all_to_all | solution.py:506
  39.4 0.0 copy-done
  39.4 0.0 copy-done.1
  39.4 1.7 %first.1 = (bf16[36,64,128]{2,1,0:T(8,128)(2,1)S(1)}, f32[8,128]{1,0:T(8,128)S(1)}, f32[32,1,1280]{2,1,0:T(1,128)S(1)}) custom-call(bf16[32,96,128]{2,1,0:T(8,128)(2,1)S(1)} %all_to_all.20.refs_0_, s32[1,512]{1,0:T(1,128)S(1)} %bitcast.5, s32[64]{0:T(128)S(1)} %copy-done.1), custom_call_target="tpu_custom_call" | custom-call | tf_op jit(solution)/shard_map/first/pallas_call | solution.py:508
  41.1 10.6 %all_to_all.21.refs_0_ = f32[32,1,1280]{2,1,0:T(1,128)S(1)} all-to-all(f32[32,1,1280]{2,1,0:T(1,128)S(1)} %get-tuple-element.13), channel_id=1, replica_groups=mesh['row'=4,'col'=8] {'row','col'}, dimensions={0} | all-to-all | bytes 327680 | tf_op jit(solution)/shard_map/all_to_all | solution.py:523
  51.7 1.4 %step.2 = (f32[3,4,8,128]{3,2,1,0:T(8,128)S(1)}, f32[32,1,1152]{2,1,0:T(1,128)S(1)}, bf16[36,64,128]{2,1,0:T(8,128)(2,1)}) custom-call(f32[32,1,1280]{2,1,0:T(1,128)S(1)} %all_to_all.21.refs_0_, bf16[36,64,128]{2,1,0:T(8,128)(2,1)S(1)} %get-tuple-element.14.refs_1_, f32[8,128]{1,0:T(8,128)S(1)} %get-tuple-element.15.refs_2_, ...), custom_call_target="tpu_custom_call" | custom-call | tf_op jit(solution)/shard_map/step/pallas_call | solution.py:535
  53.1 10.4 %all_to_all.22.refs_0_ = f32[32,1,1152]{2,1,0:T(1,128)S(1)} all-to-all(f32[32,1,1152]{2,1,0:T(1,128)S(1)} %get-tuple-element.17), channel_id=1, replica_groups=mesh['row'=4,'col'=8] {'row','col'}, dimensions={0} | all-to-all | bytes 294912 | tf_op jit(solution)/shard_map/all_to_all | solution.py:523
  63.5 1.3 %step.3 = (f32[3,4,8,128]{3,2,1,0:T(8,128)S(1)}, f32[32,1,1152]{2,1,0:T(1,128)S(1)}) custom-call(f32[32,1,1152]{2,1,0:T(1,128)S(1)} %all_to_all.22.refs_0_, bf16[36,64,128]{2,1,0:T(8,128)(2,1)S(1)} %get-tuple-element.14.refs_1_, f32[8,128]{1,0:T(8,128)S(1)} %get-tuple-element.15.refs_2_, f32[3,4,8,128]{3,2,1,0:T(8,128)S(1)} %get-tuple-element.18.refs_3_, ...), custom_call_target="tpu_custom_call" | custom-call | tf_op jit(solution)/shard_map/step/pallas_call | solution.py:535
  64.8 10.2 %all_to_all.23.refs_0_ = f32[32,1,1152]{2,1,0:T(1,128)S(1)} all-to-all(f32[32,1,1152]{2,1,0:T(1,128)S(1)} %get-tuple-element.19), channel_id=1, replica_groups=mesh['row'=4,'col'=8] {'row','col'}, dimensions={0} | all-to-all | bytes 294912 | tf_op jit(solution)/shard_map/all_to_all | solution.py:546
  75.0 0.8 %last.1 = (f32[6,128]{1,0:T(8,128)}, f32[6,128]{1,0:T(8,128)}) custom-call(f32[32,1,1152]{2,1,0:T(1,128)S(1)} %all_to_all.23.refs_0_, f32[3,4,8,128]{3,2,1,0:T(8,128)S(1)} %get-tuple-element.20.refs_1_), custom_call_target="tpu_custom_call" | custom-call | tf_op jit(solution)/shard_map/last/pallas_call | solution.py:547
  (1 shorter events, 0.0 us)
Async XLA Ops:
  10.4 29.0 %copy-start = (s32[512]{0:T(512)S(1)}, s32[512]{0:T(512)}, u32[]{:S(2)}) copy-start(s32[512]{0:T(512)} %refs_6_.1) | copy-start | bytes 6148
  10.4 29.0 %copy-start.1 = (s32[64]{0:T(128)S(1)}, s32[64]{0:T(128)}, u32[]{:S(2)}) copy-start(s32[64]{0:T(128)} %constant.4.clone.refs_2_.refs_4_) | copy-start | bytes 772

commit v3 on v2

--- a/solution.py
+++ b/solution.py
@@ -177,16 +177,17 @@
 
     for copy in wholes[1:]:
         copy.wait()
-    spots = iota((scenes, points), 0)
-
-    def scene_step(s, carry):
+    spots = iota((points, scenes), 1)
+    mates = jnp.transpose(partner_ref[...])
+
+    def scene_step(s):
         values = jnp.concatenate(
             [vals_ref.at[t][pl.ds(s, 64, stride=scn), :] for t in range(points // LANES)], axis=1
         )
         high, low = split_two(values)
         left = jnp.concatenate([high, low], axis=0)
-        onehot = jnp.where(spots == partner_ref[pl.ds(s, 1), :], 1.0, 0.0).astype(BF16)
-        both = lax.dot_general(left, onehot, CONTRACT_LAST, preferred_element_type=F32)
+        onehot = jnp.where(spots == mates[:, s : s + 1], 1.0, 0.0).astype(BF16)
+        both = jnp.dot(left, onehot, preferred_element_type=F32)
         total = both[:64] + both[64:]
         acc_ref[...] += total
         mine = map_sm[device * scn + s]
@@ -194,9 +195,9 @@
         for other in range(scn):
             rank = rank + (map_sm[device * scn + other] < mine).astype(jnp.int32)
         links_ref[pl.ds(pl.multiple_of(rank * 48, 16), 48), :] = total[:48].astype(BF16)
-        return carry
-
-    lax.fori_loop(0, scn, scene_step, 0, unroll=4)
+
+    for s in range(scn):
+        scene_step(s)
 
     lane = iota((32, LANES), 1)
     own = jnp.zeros((32, LANES), F32)
@@ -224,9 +225,10 @@
     extra_ref[base : base + 8, :] = flat_ref[0:8, :]
     extra_ref[base + 8 : base + 16, :] = flat_ref[32:40, :]
 
-    onto = jnp.where(iota((scenes, scenes), 0) == map_ref[...], 1.0, 0.0).astype(BF16)
+    places = jnp.transpose(jnp.broadcast_to(map_ref[...], (8, scenes)))[:, :1]
+    onto = jnp.where(iota((scenes, scenes), 1) == places, 1.0, 0.0).astype(BF16)
     left = jnp.concatenate([links_ref[...], extra_ref[...].astype(BF16)], axis=0)
-    perm_ref[...] = lax.dot_general(left, onto, CONTRACT_LAST, preferred_element_type=F32)
+    perm_ref[...] = jnp.dot(left, onto, preferred_element_type=F32)
 
     top = scn * 48
     first = iota((8, LANES), 1) < HALF
@@ -267,7 +269,7 @@
                     send_ref[r * col_count + c, slot * 24 : slot * 24 + 24, :] = block.astype(BF16)
 
 
-def tile_matvec(tile_ref, own_ref, rows_part, cols_part, pair_sm, rows_ref):
+def tile_matvec(tile_ref, own_ref, rows_part, cols_part, rows_ref):
     which = iota((8, LANES), 0)
     turned = jnp.transpose(cols_part)[:HALF]
     forward = [jnp.zeros((8, LANES), F32) for _ in range(6)]
@@ -292,8 +294,13 @@
     per_col = -(-21 // lax.axis_size("col"))
     for i in range(per_col):
         q = jnp.minimum(col * per_col + i, 20)
-        x = pair_sm[q]
-        y = pair_sm[32 + q]
+        x = jnp.int32(0)
+        start = jnp.int32(0)
+        for line in range(1, 6):
+            past = (q >= PAIRS.index((line, line))).astype(jnp.int32)
+            x = x + past
+            start = start + past * (7 - line)
+        y = q - start + x
         weight = own_ref[i : i + 1, :]
         at_x = rows_ref[pl.ds(x, 1), :] * weight
         at_y = rows_ref[pl.ds(y, 1), :] * weight
@@ -312,7 +319,7 @@
 
 
 def first_kernel(
-    row_count, col_count, got_ref, map_ref, pair_sm, tile_ref, own_ref, part_ref, wide_ref, rows_ref,
+    row_count, col_count, got_ref, map_ref, tile_ref, own_ref, part_ref, wide_ref, rows_ref,
 ):
     devices = got_ref.shape[0]
     scenes = map_ref.shape[1]
@@ -359,7 +366,7 @@
     rows_part = jnp.where(used, extras[0] + extras[1], 0.0)
     cols_part = jnp.where(used, extras[2] + pltpu.roll(extras[2], HALF, 1), 0.0)
     own_ref[...] = extras[3] + pltpu.roll(extras[3], 5, 0)
-    out, sides = tile_matvec(tile_ref, own_ref, rows_part, cols_part, pair_sm, rows_ref)
+    out, sides = tile_matvec(tile_ref, own_ref, rows_part, cols_part, rows_ref)
     rows_ref[...] = rows_part
     line = rows_ref[pl.ds(jnp.minimum(lax.axis_index("col"), 5), 1), :]
     write_partials(out, sides, line, part_ref)
@@ -393,7 +400,7 @@
 
 
 def step_kernel(
-    row_count, col_count, begin, got_ref, tile_ref, own_ref, state_ref, pair_sm, next_ref, part_ref,
+    row_count, col_count, begin, got_ref, tile_ref, own_ref, state_ref, next_ref, part_ref,
     *rest,
 ):
     if begin:
@@ -428,7 +435,7 @@
     wide = next_ref[2, lax.div(col, 2)]
     turned = pltpu.roll(wide, HALF, 1)
     cols_part = jnp.where(iota((8, LANES), 0) * 0 == lax.rem(col, 2), wide, turned)
-    out, sides = tile_matvec(tile_ref, own_ref, rows_part, cols_part, pair_sm, rows_ref)
+    out, sides = tile_matvec(tile_ref, own_ref, rows_part, cols_part, rows_ref)
     write_partials(out, sides, None, part_ref)
     if begin:
         copy.wait()
@@ -449,10 +456,6 @@
     return pl.BlockSpec(memory_space=pltpu.VMEM)
 
 
-def smem():
-    return pl.BlockSpec(memory_space=pltpu.SMEM)
-
-
 def hbm():
     return pl.BlockSpec(memory_space=pltpu.HBM)
 
@@ -468,7 +471,6 @@
     scenes = tile_map.shape[0]
     scn, points = partner.shape
     map_row = tile_map.reshape(1, scenes)
-    pairs = jnp.asarray([p[0] for p in PAIRS] + [0] * 11 + [p[1] for p in PAIRS] + [0] * 11, jnp.int32)
 
     def bind(kernel, *fixed):
         def run(*refs):
@@ -502,7 +504,12 @@
         ],
         compiler_params=small_limit(36),
         name="assemble",
-    )(*[pltpu.with_memory_space_constraint(v, pltpu.HBM) for v in (cam_jac, pt_jac, resid, partner, map_row, count, tile_map)])
+    )(
+        *[
+            pltpu.with_memory_space_constraint(value, pltpu.HBM)
+            for value in (cam_jac, pt_jac, resid, partner, map_row, count, tile_map)
+        ]
+    )
     got = lax.all_to_all(send, AXES, 0, 0, tiled=True)
     tile_rows = scenes // row_count
     tile, own, part = pl.pallas_call(
@@ -512,12 +519,12 @@
             jax.ShapeDtypeStruct((8, LANES), F32),
             jax.ShapeDtypeStruct((devices, 1, 10 * LANES), F32),
         ),
-        in_specs=[vmem(), vmem(), smem()],
+        in_specs=[vmem()] * 2,
         out_specs=(vmem(),) * 3,
         scratch_shapes=[pltpu.VMEM((devices * 96, LANES), F32), pltpu.VMEM((8, LANES), F32)],
         compiler_params=small_limit(16),
         name="first",
-    )(got, map_row, pairs)
+    )(got, map_row)
     state = jnp.zeros((3, row_count, 8, LANES), F32)
     for turn in range(ITERS - 1):
         got = lax.all_to_all(part, AXES, 0, 0, tiled=True)
@@ -535,12 +542,12 @@
         state, part, *rest = pl.pallas_call(
             bind(step_kernel, begin),
             out_shape=outs,
-            in_specs=[vmem()] * 4 + [smem()],
+            in_specs=[vmem()] * 4,
             out_specs=places,
             scratch_shapes=scratch,
             compiler_params=small_limit(8),
             name="step",
-        )(got, tile, own, state, pairs)
+        )(got, tile, own, state)
         if begin:
             coupling = rest[0]
     got = lax.all_to_all(part, AXES, 0, 0, tiled=True)

time: 76.1 us -> 72.7 us (0.955)
  Pallas kernels: 15 us -> 11.7 us
    pallas_call x1, Pallas kernels: 9.75 us -> 7.52 us  [packed_shards(): pl.pallas_call(bind(assemble_kernel), out_shape=jax.ShapeDtypeStruct((dev...]
where the time goes in v3:
time: 72.7 us; the launch traced here: 72.5 us
  blocking collectives  60.2 us (83%)
  Pallas kernels  11.7 us (16%)
    all_to_all x3, blocking collectives, packed_shards(): got = lax.all_to_all(part, AXES, 0, 0, tiled=True)  31.2 us
    all_to_all x1, blocking collectives, packed_shards(): got = lax.all_to_all(send, AXES, 0, 0, tiled=True)  29 us
    pallas_call x1, Pallas kernels, packed_shards(): pl.pallas_call(bind(assemble_kernel), out_shape=jax.ShapeDtypeStruct((dev...  7.52 us
    pallas_call x2, Pallas kernels, packed_shards(): pl.pallas_call(bind(step_kernel, begin), out_shape=outs, in_specs=[vmem()...  2.15 us

profile of v3, /device:TPU:0, one launch (start us, length us, event | category | flops | bytes accessed | tf_op | source)
XLA Modules:
  0.0 72.5 jit_solution(3117197880312597299)
XLA Ops:
  0.6 7.5 %assemble.1 = bf16[32,96,128]{2,1,0:T(8,128)(2,1)S(1)} custom-call(bf16[2,2,6,16,1024]{4,3,2,1,0:T(8,128)(2,1)} %refs_0_.1, bf16[2,2,3,16,1024]{4,3,2,1,0:T(8,128)(2,1)} %refs_1_.1, bf16[2,2,16,1024]{3,2,1,0:T(8,128)(2,1)} %refs_2_.1, s32[16,1024]{1,0:T(8,128)} %refs_3_.1, s32[1,512]{1,0:T(1,128)} %bitcast.4, s32[16]{0:T(128)} %refs_5_.1, s32[512]{0:T(512)} %refs_6_.1), custom_call_target="tpu_custom_call" | custom-call | tf_op jit(solution)/shard_map/assemble/pallas_call | solution.py:482
  8.2 0.0 copy-start
  8.2 29.0 %all_to_all.20.refs_0_ = bf16[32,96,128]{2,1,0:T(8,128)(2,1)S(1)} all-to-all(bf16[32,96,128]{2,1,0:T(8,128)(2,1)S(1)} %assemble.1), channel_id=1, replica_groups=mesh['row'=4,'col'=8] {'row','col'}, dimensions={0} | all-to-all | bytes 1572864 | tf_op jit(solution)/shard_map/all_to_all | solution.py:513
  37.1 0.0 copy-done
  37.2 1.1 %first.1 = (bf16[36,64,128]{2,1,0:T(8,128)(2,1)S(1)}, f32[8,128]{1,0:T(8,128)S(1)}, f32[32,1,1280]{2,1,0:T(1,128)S(1)}) custom-call(bf16[32,96,128]{2,1,0:T(8,128)(2,1)S(1)} %all_to_all.20.refs_0_, s32[1,512]{1,0:T(1,128)S(1)} %bitcast.5), custom_call_target="tpu_custom_call" | custom-call | tf_op jit(solution)/shard_map/first/pallas_call | solution.py:515
  38.3 10.6 %all_to_all.21.refs_0_ = f32[32,1,1280]{2,1,0:T(1,128)S(1)} all-to-all(f32[32,1,1280]{2,1,0:T(1,128)S(1)} %get-tuple-element.13), channel_id=1, replica_groups=mesh['row'=4,'col'=8] {'row','col'}, dimensions={0} | all-to-all | bytes 327680 | tf_op jit(solution)/shard_map/all_to_all | solution.py:530
  49.0 1.4 %step.2 = (f32[3,4,8,128]{3,2,1,0:T(8,128)S(1)}, f32[32,1,1152]{2,1,0:T(1,128)S(1)}, bf16[36,64,128]{2,1,0:T(8,128)(2,1)}) custom-call(f32[32,1,1280]{2,1,0:T(1,128)S(1)} %all_to_all.21.refs_0_, bf16[36,64,128]{2,1,0:T(8,128)(2,1)S(1)} %get-tuple-element.14.refs_1_, f32[8,128]{1,0:T(8,128)S(1)} %get-tuple-element.15.refs_2_, ...), custom_call_target="tpu_custom_call" | custom-call | tf_op jit(solution)/shard_map/step/pallas_call | solution.py:542
  50.3 10.4 %all_to_all.22.refs_0_ = f32[32,1,1152]{2,1,0:T(1,128)S(1)} all-to-all(f32[32,1,1152]{2,1,0:T(1,128)S(1)} %get-tuple-element.17), channel_id=1, replica_groups=mesh['row'=4,'col'=8] {'row','col'}, dimensions={0} | all-to-all | bytes 294912 | tf_op jit(solution)/shard_map/all_to_all | solution.py:530
  60.7 0.8 %step.3 = (f32[3,4,8,128]{3,2,1,0:T(8,128)S(1)}, f32[32,1,1152]{2,1,0:T(1,128)S(1)}) custom-call(f32[32,1,1152]{2,1,0:T(1,128)S(1)} %all_to_all.22.refs_0_, bf16[36,64,128]{2,1,0:T(8,128)(2,1)S(1)} %get-tuple-element.14.refs_1_, f32[8,128]{1,0:T(8,128)S(1)} %get-tuple-element.15.refs_2_, f32[3,4,8,128]{3,2,1,0:T(8,128)S(1)} %get-tuple-element.18.refs_3_), custom_call_target="tpu_custom_call" | custom-call | tf_op jit(solution)/shard_map/step/pallas_call | solution.py:542
  61.5 10.2 %all_to_all.23.refs_0_ = f32[32,1,1152]{2,1,0:T(1,128)S(1)} all-to-all(f32[32,1,1152]{2,1,0:T(1,128)S(1)} %get-tuple-element.19), channel_id=1, replica_groups=mesh['row'=4,'col'=8] {'row','col'}, dimensions={0} | all-to-all | bytes 294912 | tf_op jit(solution)/shard_map/all_to_all | solution.py:553
  71.7 0.8 %last.1 = (f32[6,128]{1,0:T(8,128)}, f32[6,128]{1,0:T(8,128)}) custom-call(f32[32,1,1152]{2,1,0:T(1,128)S(1)} %all_to_all.23.refs_0_, f32[3,4,8,128]{3,2,1,0:T(8,128)S(1)} %get-tuple-element.20.refs_1_), custom_call_target="tpu_custom_call" | custom-call | tf_op jit(solution)/shard_map/last/pallas_call | solution.py:554
  (1 shorter events, 0.0 us)
Async XLA Ops:
  8.2 29.0 %copy-start = (s32[512]{0:T(512)S(1)}, s32[512]{0:T(512)}, u32[]{:S(2)}) copy-start(s32[512]{0:T(512)} %refs_6_.1) | copy-start | bytes 6148

commit v4 on v3

--- a/solution.py
+++ b/solution.py
@@ -126,11 +126,12 @@
     per_group = scn // row_count
     device = lax.axis_index("row") * col_count + lax.axis_index("col")
     slab = (scn, LANES)
+    pitch = scn + 1
 
     own_ref[...] = jnp.zeros_like(own_ref)
     acc_ref[...] = jnp.zeros_like(acc_ref)
     extra_ref[...] = jnp.zeros_like(extra_ref)
-    vals_ref[:, pl.ds(63 * scn, scn), :] = jnp.zeros((points // LANES, scn, LANES), F32)
+    vals_ref[:, pl.ds(63 * pitch, scn), :] = jnp.zeros((points // LANES, scn, LANES), F32)
 
     wholes[0].wait()
     sub = iota(slab, 0)
@@ -156,10 +157,10 @@
         diag_own, diag_other, link, grad_own, grad_other = point_values(ja, jb, pa, pb, ea, eb, live)
 
         def put(q, value):
-            vals_ref[step, pl.ds(q * scn, scn), :] = value
+            vals_ref[step, pl.ds(q * pitch, scn), :] = value
 
         def put_own(q, value):
-            own_ref[pl.ds(q * scn, scn), :] += value
+            own_ref[pl.ds(q * pitch, scn), :] += value
 
         for x in range(3):
             for y in range(6):
@@ -177,16 +178,16 @@
 
     for copy in wholes[1:]:
         copy.wait()
-    spots = iota((points, scenes), 1)
-    mates = jnp.transpose(partner_ref[...])
+    spots = iota((points, scenes), 1).astype(jnp.int16)
+    mates = jnp.transpose(partner_ref[...]).astype(jnp.int16)
 
     def scene_step(s):
         values = jnp.concatenate(
-            [vals_ref.at[t][pl.ds(s, 64, stride=scn), :] for t in range(points // LANES)], axis=1
+            [vals_ref.at[t][pl.ds(s, 64, stride=pitch), :] for t in range(points // LANES)], axis=1
         )
         high, low = split_two(values)
         left = jnp.concatenate([high, low], axis=0)
-        onehot = jnp.where(spots == mates[:, s : s + 1], 1.0, 0.0).astype(BF16)
+        onehot = jnp.where(spots == mates[:, s : s + 1], jnp.asarray(1, BF16), jnp.asarray(0, BF16))
         both = jnp.dot(left, onehot, preferred_element_type=F32)
         total = both[:64] + both[64:]
         acc_ref[...] += total
@@ -202,7 +203,7 @@
     lane = iota((32, LANES), 1)
     own = jnp.zeros((32, LANES), F32)
     for s in range(scn):
-        column = jnp.sum(own_ref[pl.ds(s, 32, stride=scn), :], axis=1, keepdims=True)
+        column = jnp.sum(own_ref[pl.ds(s, 32, stride=pitch), :], axis=1, keepdims=True)
         own = own + jnp.where(lane == s, column, 0.0)
     start = device * scn
     own = pltpu.roll(own, lax.rem(start, LANES), 1)
@@ -350,17 +351,19 @@
     select = select.astype(BF16)
 
     for n in range(devices):
-        wide_ref[pl.ds(n * 96, 96), :] = got_ref[n].astype(F32)
+        block = got_ref[n].astype(F32)
+        for slot in range(per_group):
+            wide_ref[pl.ds((n * per_group + slot) * 25, 24), :] = block[slot * 24 : slot * 24 + 24]
     for k in range(18):
-        picked = wide_ref[pl.ds(k, tile_rows, stride=24), :].astype(BF16)
+        picked = wide_ref[pl.ds(k, tile_rows, stride=25), :].astype(BF16)
         block = lax.dot_general(picked, select, (((0,), (1,)), ((), ())), preferred_element_type=F32)
         tile_ref[k] = block[:HALF].astype(BF16)
         tile_ref[k + 18] = block[HALF:].astype(BF16)
     extras = []
     for slot in range(per_group):
-        total = wide_ref[slot * 24 + 16 : slot * 24 + 24, :]
+        total = got_ref[0, slot * 24 + 16 : slot * 24 + 24, :].astype(F32)
         for n in range(1, devices):
-            total = total + wide_ref[n * 96 + slot * 24 + 16 : n * 96 + slot * 24 + 24, :]
+            total = total + got_ref[n, slot * 24 + 16 : slot * 24 + 24, :].astype(F32)
         extras.append(pltpu.roll(total, 6, 0))
     used = iota((8, LANES), 0) < 6
     rows_part = jnp.where(used, extras[0] + extras[1], 0.0)
@@ -485,8 +488,8 @@
         in_specs=[hbm()] * 7,
         out_specs=vmem(),
         scratch_shapes=[
-            pltpu.VMEM((points // LANES, 64 * scn, LANES), F32),
-            pltpu.VMEM((32 * scn, LANES), F32),
+            pltpu.VMEM((points // LANES, 64 * (scn + 1), LANES), F32),
+            pltpu.VMEM((32 * (scn + 1), LANES), F32),
             pltpu.VMEM((64, scenes), F32),
             pltpu.VMEM((48 * scn, scenes), BF16),
             pltpu.VMEM((64, scenes), F32),
@@ -521,7 +524,7 @@
         ),
         in_specs=[vmem()] * 2,
         out_specs=(vmem(),) * 3,
-        scratch_shapes=[pltpu.VMEM((devices * 96, LANES), F32), pltpu.VMEM((8, LANES), F32)],
+        scratch_shapes=[pltpu.VMEM((tile_rows * 25, LANES), F32), pltpu.VMEM((8, LANES), F32)],
         compiler_params=small_limit(16),
         name="first",
     )(got, map_row)

time: 72.7 us -> 71.5 us (0.983)
  Pallas kernels: 11.7 us -> 10.4 us
    pallas_call x1, Pallas kernels: 7.52 us -> 6.33 us  [packed_shards(): pl.pallas_call(bind(assemble_kernel), out_shape=jax.ShapeDtypeStruct((dev...]
where the time goes in v4:
time: 71.5 us; the launch traced here: 71.3 us
  blocking collectives  60.2 us (84%)
  Pallas kernels  10.4 us (15%)
    all_to_all x3, blocking collectives, packed_shards(): got = lax.all_to_all(part, AXES, 0, 0, tiled=True)  31.2 us
    all_to_all x1, blocking collectives, packed_shards(): got = lax.all_to_all(send, AXES, 0, 0, tiled=True)  29 us
    pallas_call x1, Pallas kernels, packed_shards(): pl.pallas_call(bind(assemble_kernel), out_shape=jax.ShapeDtypeStruct((dev...  6.33 us
    pallas_call x2, Pallas kernels, packed_shards(): pl.pallas_call(bind(step_kernel, begin), out_shape=outs, in_specs=[vmem()...  2.15 us

profile of v4, /device:TPU:0, one launch (start us, length us, event | category | flops | bytes accessed | tf_op | source)
XLA Modules:
  0.0 71.3 jit_solution(3442851861187929233)
XLA Ops:
  0.6 6.3 %assemble.1 = bf16[32,96,128]{2,1,0:T(8,128)(2,1)S(1)} custom-call(bf16[2,2,6,16,1024]{4,3,2,1,0:T(8,128)(2,1)} %refs_0_.1, bf16[2,2,3,16,1024]{4,3,2,1,0:T(8,128)(2,1)} %refs_1_.1, bf16[2,2,16,1024]{3,2,1,0:T(8,128)(2,1)} %refs_2_.1, s32[16,1024]{1,0:T(8,128)} %refs_3_.1, s32[1,512]{1,0:T(1,128)} %bitcast.4, s32[16]{0:T(128)} %refs_5_.1, s32[512]{0:T(512)} %refs_6_.1), custom_call_target="tpu_custom_call" | custom-call | tf_op jit(solution)/shard_map/assemble/pallas_call | solution.py:485
  7.0 0.0 copy-start
  7.0 29.0 %all_to_all.20.refs_0_ = bf16[32,96,128]{2,1,0:T(8,128)(2,1)S(1)} all-to-all(bf16[32,96,128]{2,1,0:T(8,128)(2,1)S(1)} %assemble.1), channel_id=1, replica_groups=mesh['row'=4,'col'=8] {'row','col'}, dimensions={0} | all-to-all | bytes 1572864 | tf_op jit(solution)/shard_map/all_to_all | solution.py:516
  36.0 0.0 copy-done
  36.0 1.1 %first.1 = (bf16[36,64,128]{2,1,0:T(8,128)(2,1)S(1)}, f32[8,128]{1,0:T(8,128)S(1)}, f32[32,1,1280]{2,1,0:T(1,128)S(1)}) custom-call(bf16[32,96,128]{2,1,0:T(8,128)(2,1)S(1)} %all_to_all.20.refs_0_, s32[1,512]{1,0:T(1,128)S(1)} %bitcast.5), custom_call_target="tpu_custom_call" | custom-call | tf_op jit(solution)/shard_map/first/pallas_call | solution.py:518
  37.1 10.6 %all_to_all.21.refs_0_ = f32[32,1,1280]{2,1,0:T(1,128)S(1)} all-to-all(f32[32,1,1280]{2,1,0:T(1,128)S(1)} %get-tuple-element.13), channel_id=1, replica_groups=mesh['row'=4,'col'=8] {'row','col'}, dimensions={0} | all-to-all | bytes 327680 | tf_op jit(solution)/shard_map/all_to_all | solution.py:533
  47.8 1.4 %step.2 = (f32[3,4,8,128]{3,2,1,0:T(8,128)S(1)}, f32[32,1,1152]{2,1,0:T(1,128)S(1)}, bf16[36,64,128]{2,1,0:T(8,128)(2,1)}) custom-call(f32[32,1,1280]{2,1,0:T(1,128)S(1)} %all_to_all.21.refs_0_, bf16[36,64,128]{2,1,0:T(8,128)(2,1)S(1)} %get-tuple-element.14.refs_1_, f32[8,128]{1,0:T(8,128)S(1)} %get-tuple-element.15.refs_2_, ...), custom_call_target="tpu_custom_call" | custom-call | tf_op jit(solution)/shard_map/step/pallas_call | solution.py:545
  49.1 10.4 %all_to_all.22.refs_0_ = f32[32,1,1152]{2,1,0:T(1,128)S(1)} all-to-all(f32[32,1,1152]{2,1,0:T(1,128)S(1)} %get-tuple-element.17), channel_id=1, replica_groups=mesh['row'=4,'col'=8] {'row','col'}, dimensions={0} | all-to-all | bytes 294912 | tf_op jit(solution)/shard_map/all_to_all | solution.py:533
  59.5 0.8 %step.3 = (f32[3,4,8,128]{3,2,1,0:T(8,128)S(1)}, f32[32,1,1152]{2,1,0:T(1,128)S(1)}) custom-call(f32[32,1,1152]{2,1,0:T(1,128)S(1)} %all_to_all.22.refs_0_, bf16[36,64,128]{2,1,0:T(8,128)(2,1)S(1)} %get-tuple-element.14.refs_1_, f32[8,128]{1,0:T(8,128)S(1)} %get-tuple-element.15.refs_2_, f32[3,4,8,128]{3,2,1,0:T(8,128)S(1)} %get-tuple-element.18.refs_3_), custom_call_target="tpu_custom_call" | custom-call | tf_op jit(solution)/shard_map/step/pallas_call | solution.py:545
  60.3 10.2 %all_to_all.23.refs_0_ = f32[32,1,1152]{2,1,0:T(1,128)S(1)} all-to-all(f32[32,1,1152]{2,1,0:T(1,128)S(1)} %get-tuple-element.19), channel_id=1, replica_groups=mesh['row'=4,'col'=8] {'row','col'}, dimensions={0} | all-to-all | bytes 294912 | tf_op jit(solution)/shard_map/all_to_all | solution.py:556
  70.5 0.8 %last.1 = (f32[6,128]{1,0:T(8,128)}, f32[6,128]{1,0:T(8,128)}) custom-call(f32[32,1,1152]{2,1,0:T(1,128)S(1)} %all_to_all.23.refs_0_, f32[3,4,8,128]{3,2,1,0:T(8,128)S(1)} %get-tuple-element.20.refs_1_), custom_call_target="tpu_custom_call" | custom-call | tf_op jit(solution)/shard_map/last/pallas_call | solution.py:557
  (1 shorter events, 0.0 us)
Async XLA Ops:
  7.0 29.0 %copy-start = (s32[512]{0:T(512)S(1)}, s32[512]{0:T(512)}, u32[]{:S(2)}) copy-start(s32[512]{0:T(512)} %refs_6_.1) | copy-start | bytes 6148

commit v5 on v4

--- a/solution.py
+++ b/solution.py
@@ -93,8 +93,36 @@
     return diag_own, diag_other, link, grad_own, grad_other
 
 
+def selection(row_count, map_ref, scn, tile_rows, per_group):
+    scenes = map_ref.shape[1]
+    row = lax.axis_index("row")
+    tiles = jnp.concatenate(
+        [map_ref[:, t * LANES : (t + 1) * LANES] for t in range(scenes // LANES)], axis=0
+    )
+    groups = scenes // LANES
+    place = iota((groups, LANES), 1) % scn
+    rank = jnp.zeros((groups, LANES), jnp.int32)
+    for shift in range(1, scn):
+        before = pltpu.roll(tiles, shift, 1)
+        after = pltpu.roll(tiles, LANES - shift, 1)
+        rank = rank + ((before < tiles) & (place >= shift)).astype(jnp.int32)
+        rank = rank + ((after < tiles) & (place + shift < scn)).astype(jnp.int32)
+    scene_id = iota((groups, LANES), 0) * LANES + iota((groups, LANES), 1)
+    slot_at = (scene_id // scn) * 8 + rank % per_group
+    local = tiles - row * tile_rows
+    slot_at = jnp.where((local >= 0) & (local < tile_rows), slot_at, -1)
+    deep = scenes // scn * 8
+    select = jnp.zeros((deep, tile_rows), F32)
+    for t in range(groups):
+        to_row = jnp.where(iota((tile_rows, LANES), 0) == local[t : t + 1, :], 1.0, 0.0).astype(BF16)
+        from_slot = jnp.where(iota((deep, LANES), 0) == slot_at[t : t + 1, :], 1.0, 0.0).astype(BF16)
+        select = select + lax.dot_general(from_slot, to_row, CONTRACT_LAST, preferred_element_type=F32)
+    return jnp.concatenate([select, pltpu.roll(select, 4, 0)], axis=1).astype(BF16)
+
+
 def assemble_kernel(
     row_count, col_count, cam_in, pt_in, res_in, partner_in, row_in, count_in, map_in, send_ref,
+    select_ref,
     vals_ref, own_ref, acc_ref, links_ref, flat_ref, extra_ref, perm_ref,
     cam_ref, pt_ref, res_ref, partner_ref, map_ref, count_sm, map_sm, slab_sem, whole_sem,
 ):
@@ -178,6 +206,7 @@
 
     for copy in wholes[1:]:
         copy.wait()
+    select_ref[...] = selection(row_count, map_ref, scn, scenes // row_count, per_group)
     spots = iota((points, scenes), 1).astype(jnp.int16)
     mates = jnp.transpose(partner_ref[...]).astype(jnp.int16)
 
@@ -195,7 +224,11 @@
         rank = jnp.int32(0)
         for other in range(scn):
             rank = rank + (map_sm[device * scn + other] < mine).astype(jnp.int32)
-        links_ref[pl.ds(pl.multiple_of(rank * 48, 16), 48), :] = total[:48].astype(BF16)
+        base = lax.div(rank, per_group) * (36 * per_group) + lax.rem(rank, per_group)
+        for t in range(scenes // LANES):
+            cols = slice(t * LANES, (t + 1) * LANES)
+            links_ref.at[t][pl.ds(base, 18, stride=per_group), :] = total[0:18, cols]
+            links_ref.at[t][pl.ds(base + 18 * per_group, 18, stride=per_group), :] = total[24:42, cols]
 
     for s in range(scn):
         scene_step(s)
@@ -220,54 +253,47 @@
         for i in range(per_col):
             q = c * per_col + i
             if q < 21:
-                extra_ref[c * 8 + 2 + i : c * 8 + 3 + i, :] = flat_ref[10 + q : 11 + q, :]
-                extra_ref[c * 8 + 5 + i : c * 8 + 6 + i, :] = flat_ref[42 + q : 43 + q, :]
+                extra_ref[c * 8 + 2 * i : c * 8 + 2 * i + 1, :] = flat_ref[10 + q : 11 + q, :]
+                extra_ref[c * 8 + 2 * i + 1 : c * 8 + 2 * i + 2, :] = flat_ref[42 + q : 43 + q, :]
     base = col_count * 8
     extra_ref[base : base + 8, :] = flat_ref[0:8, :]
     extra_ref[base + 8 : base + 16, :] = flat_ref[32:40, :]
 
     places = jnp.transpose(jnp.broadcast_to(map_ref[...], (8, scenes)))[:, :1]
     onto = jnp.where(iota((scenes, scenes), 1) == places, 1.0, 0.0).astype(BF16)
-    left = jnp.concatenate([links_ref[...], extra_ref[...].astype(BF16)], axis=0)
+    links = jnp.concatenate([links_ref[t] for t in range(scenes // LANES)], axis=1)
+    left = jnp.concatenate([links.astype(BF16), extra_ref[...].astype(BF16)], axis=0)
     perm_ref[...] = jnp.dot(left, onto, preferred_element_type=F32)
 
-    top = scn * 48
+    top = scn * 36
+    side = 18 * per_group
     first = iota((8, LANES), 1) < HALF
-    keep_rows = iota((8, LANES), 0) < 2
-    first24 = iota((24, LANES), 1) < HALF
+    head_rows = iota((8, LANES), 0) < 2
+    first_side = iota((side, LANES), 1) < HALF
 
     def merge(low_part, high_part, mask):
         even = jnp.where(mask, low_part, pltpu.roll(high_part, HALF, 1))
         odd = jnp.where(mask, pltpu.roll(low_part, HALF, 1), high_part)
         return even, odd
 
+    grads = [pl.ds(top + base + 8 * k, 8) for k in range(2)]
     for j in range(col_count // 2):
         cols = pl.ds(j * LANES, LANES)
-        grad_cols = merge(
-            perm_ref[top + base : top + base + 8, cols],
-            perm_ref[top + base + 8 : top + base + 16, cols],
-            first,
-        )
+        grad_cols = merge(perm_ref[grads[0], cols], perm_ref[grads[1], cols], first)
         for r in range(row_count):
             rows = pl.ds(r * LANES, LANES)
-            grad_high = perm_ref[top + base : top + base + 8, rows]
-            grad_low = perm_ref[top + base + 8 : top + base + 16, rows]
-            for slot in range(per_group):
-                at = (r * per_group + slot) * 48
-                pieces = merge(perm_ref[at : at + 24, cols], perm_ref[at + 24 : at + 48, cols], first24)
-                for k in range(2):
-                    c = 2 * j + k
-                    if slot == 0:
-                        extra = grad_high
-                    elif slot == 1:
-                        extra = grad_low
-                    elif slot == 2:
-                        extra = grad_cols[k]
-                    else:
-                        extra = perm_ref[top + c * 8 : top + c * 8 + 8, rows]
-                    tail = jnp.where(keep_rows, pieces[k][16:24], extra)
-                    block = jnp.concatenate([pieces[k][0:16], tail], axis=0)
-                    send_ref[r * col_count + c, slot * 24 : slot * 24 + 24, :] = block.astype(BF16)
+            at = r * 2 * side
+            pieces = merge(perm_ref[at : at + side, cols], perm_ref[at + side : at + 2 * side, cols], first_side)
+            for k in range(2):
+                c = 2 * j + k
+                spot = r * col_count + c
+                send_ref[spot, 0:side, :] = pieces[k].astype(BF16)
+                own = perm_ref[top + c * 8 : top + c * 8 + 8, rows]
+                tails = [perm_ref[grads[0], rows], perm_ref[grads[1], rows], grad_cols[k]]
+                for i, tail in enumerate(tails):
+                    turned = own if i == 0 else pltpu.roll(own, 8 - 2 * i, 0)
+                    block = jnp.where(head_rows, turned, tail)
+                    send_ref[spot, side + 8 * i : side + 8 * i + 8, :] = block.astype(BF16)
 
 
 def tile_matvec(tile_ref, own_ref, rows_part, cols_part, rows_ref):
@@ -320,55 +346,31 @@
 
 
 def first_kernel(
-    row_count, col_count, got_ref, map_ref, tile_ref, own_ref, part_ref, wide_ref, rows_ref,
+    row_count, col_count, got_ref, select_ref, tile_ref, own_ref, part_ref, rows_ref,
 ):
     devices = got_ref.shape[0]
-    scenes = map_ref.shape[1]
-    scn = scenes // devices
-    per_group = scn // row_count
-    tile_rows = scenes // row_count
-    row = lax.axis_index("row")
-    tiles = jnp.concatenate(
-        [map_ref[:, t * LANES : (t + 1) * LANES] for t in range(scenes // LANES)], axis=0
-    )
-    groups = scenes // LANES
-    place = iota((groups, LANES), 1) % scn
-    rank = jnp.zeros((groups, LANES), jnp.int32)
-    for shift in range(1, scn):
-        before = pltpu.roll(tiles, shift, 1)
-        after = pltpu.roll(tiles, LANES - shift, 1)
-        rank = rank + ((before < tiles) & (place >= shift)).astype(jnp.int32)
-        rank = rank + ((after < tiles) & (place + shift < scn)).astype(jnp.int32)
-    scene_id = iota((groups, LANES), 0) * LANES + iota((groups, LANES), 1)
-    slot_at = (scene_id // scn) * per_group + rank % per_group
-    local = tiles - row * tile_rows
-    slot_at = jnp.where((local >= 0) & (local < tile_rows), slot_at, -1)
-    select = jnp.zeros((tile_rows, tile_rows), F32)
-    for t in range(groups):
-        to_row = jnp.where(iota((tile_rows, LANES), 0) == local[t : t + 1, :], 1.0, 0.0).astype(BF16)
-        from_slot = jnp.where(iota((tile_rows, LANES), 0) == slot_at[t : t + 1, :], 1.0, 0.0).astype(BF16)
-        select = select + lax.dot_general(to_row, from_slot, CONTRACT_LAST, preferred_element_type=F32)
-    select = select.astype(BF16)
-
-    for n in range(devices):
-        block = got_ref[n].astype(F32)
-        for slot in range(per_group):
-            wide_ref[pl.ds((n * per_group + slot) * 25, 24), :] = block[slot * 24 : slot * 24 + 24]
-    for k in range(18):
-        picked = wide_ref[pl.ds(k, tile_rows, stride=25), :].astype(BF16)
-        block = lax.dot_general(picked, select, (((0,), (1,)), ((), ())), preferred_element_type=F32)
-        tile_ref[k] = block[:HALF].astype(BF16)
-        tile_ref[k + 18] = block[HALF:].astype(BF16)
+    deep, tile_rows = select_ref.shape[0], select_ref.shape[1] // 2
+    per_group = tile_rows // devices
+    select = select_ref[...]
+    for k in range(9):
+        picked = got_ref[:, k * 8 : k * 8 + 8, :].reshape(deep, LANES)
+        block = lax.dot_general(picked, select, (((0,), (0,)), ((), ())), preferred_element_type=F32)
+        block = block.astype(BF16)
+        for e in range(2):
+            cols = slice(e * tile_rows, (e + 1) * tile_rows)
+            tile_ref[2 * k + e] = block[:HALF, cols]
+            tile_ref[2 * k + e + 18] = block[HALF:, cols]
     extras = []
-    for slot in range(per_group):
-        total = got_ref[0, slot * 24 + 16 : slot * 24 + 24, :].astype(F32)
+    for i in range(3):
+        rows = pl.ds(18 * per_group + 8 * i, 8)
+        total = got_ref[0, rows, :].astype(F32)
         for n in range(1, devices):
-            total = total + got_ref[n, slot * 24 + 16 : slot * 24 + 24, :].astype(F32)
+            total = total + got_ref[n, rows, :].astype(F32)
+        own_ref[i : i + 1, :] = total[0:1] + total[1:2]
         extras.append(pltpu.roll(total, 6, 0))
     used = iota((8, LANES), 0) < 6
     rows_part = jnp.where(used, extras[0] + extras[1], 0.0)
     cols_part = jnp.where(used, extras[2] + pltpu.roll(extras[2], HALF, 1), 0.0)
-    own_ref[...] = extras[3] + pltpu.roll(extras[3], 5, 0)
     out, sides = tile_matvec(tile_ref, own_ref, rows_part, cols_part, rows_ref)
     rows_ref[...] = rows_part
     line = rows_ref[pl.ds(jnp.minimum(lax.axis_index("col"), 5), 1), :]
@@ -482,19 +484,23 @@
         return run
 
     extra_rows = col_count * 8 + 16
-    send = pl.pallas_call(
+    tile_rows = scenes // row_count
+    send, select = pl.pallas_call(
         bind(assemble_kernel),
-        out_shape=jax.ShapeDtypeStruct((devices, 96, LANES), BF16),
+        out_shape=(
+            jax.ShapeDtypeStruct((devices, 96, LANES), BF16),
+            jax.ShapeDtypeStruct((devices * 8, 2 * tile_rows), BF16),
+        ),
         in_specs=[hbm()] * 7,
-        out_specs=vmem(),
+        out_specs=(vmem(),) * 2,
         scratch_shapes=[
             pltpu.VMEM((points // LANES, 64 * (scn + 1), LANES), F32),
             pltpu.VMEM((32 * (scn + 1), LANES), F32),
             pltpu.VMEM((64, scenes), F32),
-            pltpu.VMEM((48 * scn, scenes), BF16),
+            pltpu.VMEM((scenes // LANES, 36 * scn, LANES), F32),
             pltpu.VMEM((64, scenes), F32),
             pltpu.VMEM((extra_rows, scenes), F32),
-            pltpu.VMEM((48 * scn + extra_rows, scenes), F32),
+            pltpu.VMEM((36 * scn + extra_rows, scenes), F32),
             pltpu.VMEM(cam_jac.shape, BF16),
             pltpu.VMEM(pt_jac.shape, BF16),
             pltpu.VMEM(resid.shape, BF16),
@@ -514,7 +520,6 @@
         ]
     )
     got = lax.all_to_all(send, AXES, 0, 0, tiled=True)
-    tile_rows = scenes // row_count
     tile, own, part = pl.pallas_call(
         bind(first_kernel),
         out_shape=(
@@ -524,10 +529,10 @@
         ),
         in_specs=[vmem()] * 2,
         out_specs=(vmem(),) * 3,
-        scratch_shapes=[pltpu.VMEM((tile_rows * 25, LANES), F32), pltpu.VMEM((8, LANES), F32)],
+        scratch_shapes=[pltpu.VMEM((8, LANES), F32)],
         compiler_params=small_limit(16),
         name="first",
-    )(got, map_row)
+    )(got, select)
     state = jnp.zeros((3, row_count, 8, LANES), F32)
     for turn in range(ITERS - 1):
         got = lax.all_to_all(part, AXES, 0, 0, tiled=True)

time: 71.5 us -> 71.1 us (level)
  no operation moved by 1% of the time
where the time goes in v5:
time: 71.1 us; the launch traced here: 70.9 us
  blocking collectives  60.2 us (85%)
  Pallas kernels  10.1 us (14%)
    all_to_all x3, blocking collectives, packed_shards(): got = lax.all_to_all(part, AXES, 0, 0, tiled=True)  31.2 us
    all_to_all x1, blocking collectives, packed_shards(): got = lax.all_to_all(send, AXES, 0, 0, tiled=True)  29 us
    pallas_call x1, Pallas kernels, packed_shards(): pl.pallas_call(bind(assemble_kernel), out_shape=(jax.ShapeDtypeStruct((de...  6.47 us
    pallas_call x2, Pallas kernels, packed_shards(): pl.pallas_call(bind(step_kernel, begin), out_shape=outs, in_specs=[vmem()...  2.15 us

profile of v5, /device:TPU:0, one launch (start us, length us, event | category | flops | bytes accessed | tf_op | source)
XLA Modules:
  0.0 70.9 jit_solution(7832047015077080747)
XLA Ops:
  0.6 6.5 %assemble.1 = (bf16[32,96,128]{2,1,0:T(8,128)(2,1)S(1)}, bf16[256,256]{1,0:T(8,128)(2,1)S(1)}) custom-call(bf16[2,2,6,16,1024]{4,3,2,1,0:T(8,128)(2,1)} %refs_0_.1, bf16[2,2,3,16,1024]{4,3,2,1,0:T(8,128)(2,1)} %refs_1_.1, bf16[2,2,16,1024]{3,2,1,0:T(8,128)(2,1)} %refs_2_.1, s32[16,1024]{1,0:T(8,128)} %refs_3_.1, s32[1,512]{1,0:T(1,128)} %bitcast.4, ...), custom_call_target="tpu_custom_call" | custom-call | tf_op jit(solution)/shard_map/assemble/pallas_call | solution.py:488
  7.1 29.0 %all_to_all.20.refs_0_ = bf16[32,96,128]{2,1,0:T(8,128)(2,1)S(1)} all-to-all(bf16[32,96,128]{2,1,0:T(8,128)(2,1)S(1)} %get-tuple-element.15), channel_id=1, replica_groups=mesh['row'=4,'col'=8] {'row','col'}, dimensions={0} | all-to-all | bytes 1572864 | tf_op jit(solution)/shard_map/all_to_all | solution.py:522
  36.1 0.6 first.1
  36.7 10.6 %all_to_all.21.refs_0_ = f32[32,1,1280]{2,1,0:T(1,128)S(1)} all-to-all(f32[32,1,1280]{2,1,0:T(1,128)S(1)} %get-tuple-element.17), channel_id=1, replica_groups=mesh['row'=4,'col'=8] {'row','col'}, dimensions={0} | all-to-all | bytes 327680 | tf_op jit(solution)/shard_map/all_to_all | solution.py:538
  47.4 1.4 %step.2 = (f32[3,4,8,128]{3,2,1,0:T(8,128)S(1)}, f32[32,1,1152]{2,1,0:T(1,128)S(1)}, bf16[36,64,128]{2,1,0:T(8,128)(2,1)}) custom-call(f32[32,1,1280]{2,1,0:T(1,128)S(1)} %all_to_all.21.refs_0_, bf16[36,64,128]{2,1,0:T(8,128)(2,1)S(1)} %get-tuple-element.18.refs_1_, f32[8,128]{1,0:T(8,128)S(1)} %get-tuple-element.19.refs_2_, ...), custom_call_target="tpu_custom_call" | custom-call | tf_op jit(solution)/shard_map/step/pallas_call | solution.py:550
  48.8 10.4 %all_to_all.22.refs_0_ = f32[32,1,1152]{2,1,0:T(1,128)S(1)} all-to-all(f32[32,1,1152]{2,1,0:T(1,128)S(1)} %get-tuple-element.21), channel_id=1, replica_groups=mesh['row'=4,'col'=8] {'row','col'}, dimensions={0} | all-to-all | bytes 294912 | tf_op jit(solution)/shard_map/all_to_all | solution.py:538
  59.1 0.8 %step.3 = (f32[3,4,8,128]{3,2,1,0:T(8,128)S(1)}, f32[32,1,1152]{2,1,0:T(1,128)S(1)}) custom-call(f32[32,1,1152]{2,1,0:T(1,128)S(1)} %all_to_all.22.refs_0_, bf16[36,64,128]{2,1,0:T(8,128)(2,1)S(1)} %get-tuple-element.18.refs_1_, f32[8,128]{1,0:T(8,128)S(1)} %get-tuple-element.19.refs_2_, f32[3,4,8,128]{3,2,1,0:T(8,128)S(1)} %get-tuple-element.22.refs_3_), custom_call_target="tpu_custom_call" | custom-call | tf_op jit(solution)/shard_map/step/pallas_call | solution.py:550
  59.9 10.2 %all_to_all.23.refs_0_ = f32[32,1,1152]{2,1,0:T(1,128)S(1)} all-to-all(f32[32,1,1152]{2,1,0:T(1,128)S(1)} %get-tuple-element.23), channel_id=1, replica_groups=mesh['row'=4,'col'=8] {'row','col'}, dimensions={0} | all-to-all | bytes 294912 | tf_op jit(solution)/shard_map/all_to_all | solution.py:561
  70.1 0.8 %last.1 = (f32[6,128]{1,0:T(8,128)}, f32[6,128]{1,0:T(8,128)}) custom-call(f32[32,1,1152]{2,1,0:T(1,128)S(1)} %all_to_all.23.refs_0_, f32[3,4,8,128]{3,2,1,0:T(8,128)S(1)} %get-tuple-element.24.refs_1_), custom_call_target="tpu_custom_call" | custom-call | tf_op jit(solution)/shard_map/last/pallas_call | solution.py:562
  (1 shorter events, 0.0 us)

commit v6 on v5

--- a/solution.py
+++ b/solution.py
@@ -137,7 +137,7 @@
     ]
 
     def slab_copies(step):
-        lanes = pl.ds(pl.multiple_of(step * LANES, LANES), LANES)
+        lanes = pl.ds(step * LANES, LANES)
         return [
             pltpu.make_async_copy(
                 source.at[..., lanes], target.at[..., lanes], slab_sem.at[k, step]
@@ -167,10 +167,10 @@
     for s in range(scn):
         counts = jnp.where(sub == s, count_sm[s], counts)
 
-    def slab_step(step, carry):
+    def slab_step(step):
         for copy in slab_copies(step):
             copy.wait()
-        lanes = pl.ds(pl.multiple_of(step * LANES, LANES), LANES)
+        lanes = pl.ds(step * LANES, LANES)
 
         def get(ref, *where):
             return ref[where + (slice(None), lanes)].astype(F32)
@@ -200,9 +200,9 @@
         for q in range(21):
             put(42 + q, diag_other[q])
             put_own(10 + q, diag_own[q])
-        return carry
-
-    lax.fori_loop(0, points // LANES, slab_step, 0)
+
+    for step in range(points // LANES):
+        slab_step(step)
 
     for copy in wholes[1:]:
         copy.wait()

time: 71.1 us -> 71 us (level)
  no operation moved by 1% of the time
where the time goes in v6:
time: 71 us; the launch traced here: 70.8 us
  blocking collectives  60.2 us (85%)
  Pallas kernels  9.99 us (14%)
    all_to_all x3, blocking collectives, packed_shards(): got = lax.all_to_all(part, AXES, 0, 0, tiled=True)  31.2 us
    all_to_all x1, blocking collectives, packed_shards(): got = lax.all_to_all(send, AXES, 0, 0, tiled=True)  29 us
    pallas_call x1, Pallas kernels, packed_shards(): pl.pallas_call(bind(assemble_kernel), out_shape=(jax.ShapeDtypeStruct((de...  6.38 us
    pallas_call x2, Pallas kernels, packed_shards(): pl.pallas_call(bind(step_kernel, begin), out_shape=outs, in_specs=[vmem()...  2.15 us

profile of v6, /device:TPU:0, one launch (start us, length us, event | category | flops | bytes accessed | tf_op | source)
XLA Modules:
  0.0 70.8 jit_solution(16402966864256717126)
XLA Ops:
  0.6 6.4 %assemble.1 = (bf16[32,96,128]{2,1,0:T(8,128)(2,1)S(1)}, bf16[256,256]{1,0:T(8,128)(2,1)S(1)}) custom-call(bf16[2,2,6,16,1024]{4,3,2,1,0:T(8,128)(2,1)} %refs_0_.1, bf16[2,2,3,16,1024]{4,3,2,1,0:T(8,128)(2,1)} %refs_1_.1, bf16[2,2,16,1024]{3,2,1,0:T(8,128)(2,1)} %refs_2_.1, s32[16,1024]{1,0:T(8,128)} %refs_3_.1, s32[1,512]{1,0:T(1,128)} %bitcast.4, ...), custom_call_target="tpu_custom_call" | custom-call | tf_op jit(solution)/shard_map/assemble/pallas_call | solution.py:488
  7.0 29.0 %all_to_all.20.refs_0_ = bf16[32,96,128]{2,1,0:T(8,128)(2,1)S(1)} all-to-all(bf16[32,96,128]{2,1,0:T(8,128)(2,1)S(1)} %get-tuple-element.15), channel_id=1, replica_groups=mesh['row'=4,'col'=8] {'row','col'}, dimensions={0} | all-to-all | bytes 1572864 | tf_op jit(solution)/shard_map/all_to_all | solution.py:522
  36.0 0.6 first.1
  36.6 10.6 %all_to_all.21.refs_0_ = f32[32,1,1280]{2,1,0:T(1,128)S(1)} all-to-all(f32[32,1,1280]{2,1,0:T(1,128)S(1)} %get-tuple-element.17), channel_id=1, replica_groups=mesh['row'=4,'col'=8] {'row','col'}, dimensions={0} | all-to-all | bytes 327680 | tf_op jit(solution)/shard_map/all_to_all | solution.py:538
  47.3 1.4 %step.2 = (f32[3,4,8,128]{3,2,1,0:T(8,128)S(1)}, f32[32,1,1152]{2,1,0:T(1,128)S(1)}, bf16[36,64,128]{2,1,0:T(8,128)(2,1)}) custom-call(f32[32,1,1280]{2,1,0:T(1,128)S(1)} %all_to_all.21.refs_0_, bf16[36,64,128]{2,1,0:T(8,128)(2,1)S(1)} %get-tuple-element.18.refs_1_, f32[8,128]{1,0:T(8,128)S(1)} %get-tuple-element.19.refs_2_, ...), custom_call_target="tpu_custom_call" | custom-call | tf_op jit(solution)/shard_map/step/pallas_call | solution.py:550
  48.7 10.4 %all_to_all.22.refs_0_ = f32[32,1,1152]{2,1,0:T(1,128)S(1)} all-to-all(f32[32,1,1152]{2,1,0:T(1,128)S(1)} %get-tuple-element.21), channel_id=1, replica_groups=mesh['row'=4,'col'=8] {'row','col'}, dimensions={0} | all-to-all | bytes 294912 | tf_op jit(solution)/shard_map/all_to_all | solution.py:538
  59.0 0.8 %step.3 = (f32[3,4,8,128]{3,2,1,0:T(8,128)S(1)}, f32[32,1,1152]{2,1,0:T(1,128)S(1)}) custom-call(f32[32,1,1152]{2,1,0:T(1,128)S(1)} %all_to_all.22.refs_0_, bf16[36,64,128]{2,1,0:T(8,128)(2,1)S(1)} %get-tuple-element.18.refs_1_, f32[8,128]{1,0:T(8,128)S(1)} %get-tuple-element.19.refs_2_, f32[3,4,8,128]{3,2,1,0:T(8,128)S(1)} %get-tuple-element.22.refs_3_), custom_call_target="tpu_custom_call" | custom-call | tf_op jit(solution)/shard_map/step/pallas_call | solution.py:550
  59.8 10.2 %all_to_all.23.refs_0_ = f32[32,1,1152]{2,1,0:T(1,128)S(1)} all-to-all(f32[32,1,1152]{2,1,0:T(1,128)S(1)} %get-tuple-element.23), channel_id=1, replica_groups=mesh['row'=4,'col'=8] {'row','col'}, dimensions={0} | all-to-all | bytes 294912 | tf_op jit(solution)/shard_map/all_to_all | solution.py:561
  70.0 0.8 %last.1 = (f32[6,128]{1,0:T(8,128)}, f32[6,128]{1,0:T(8,128)}) custom-call(f32[32,1,1152]{2,1,0:T(1,128)S(1)} %all_to_all.23.refs_0_, f32[3,4,8,128]{3,2,1,0:T(8,128)S(1)} %get-tuple-element.24.refs_1_), custom_call_target="tpu_custom_call" | custom-call | tf_op jit(solution)/shard_map/last/pallas_call | solution.py:562
  (1 shorter events, 0.0 us)

commit v7 on v5

--- a/solution.py
+++ b/solution.py
@@ -410,8 +410,17 @@
 ):
     if begin:
         coupling_ref, image_ref, rows_ref, copy_sem = rest
-        copy = pltpu.make_async_copy(tile_ref, coupling_ref, copy_sem)
-        copy.start()
+        quarter = tile_ref.shape[0] // 4
+        copies = [
+            pltpu.make_async_copy(
+                tile_ref.at[pl.ds(k * quarter, quarter)],
+                coupling_ref.at[pl.ds(k * quarter, quarter)],
+                copy_sem.at[k],
+            )
+            for k in range(4)
+        ]
+        for copy in copies:
+            copy.start()
     else:
         image_ref, rows_ref = rest
     gather_image(row_count, col_count, got_ref, image_ref)
@@ -443,7 +452,8 @@
     out, sides = tile_matvec(tile_ref, own_ref, rows_part, cols_part, rows_ref)
     write_partials(out, sides, None, part_ref)
     if begin:
-        copy.wait()
+        for copy in copies:
+            copy.wait()
 
 
 def last_kernel(row_count, col_count, got_ref, state_ref, answer_ref, remainder_ref, image_ref):
@@ -546,7 +556,7 @@
         if begin:
             outs.append(jax.ShapeDtypeStruct(tile.shape, BF16))
             places.append(hbm())
-            scratch.append(pltpu.SemaphoreType.DMA(()))
+            scratch.append(pltpu.SemaphoreType.DMA((4,)))
         state, part, *rest = pl.pallas_call(
             bind(step_kernel, begin),
             out_shape=outs,

time: 71.1 us -> 71.2 us (level)
  no operation moved by 1% of the time
where the time goes in v7:
time: 71.2 us; the launch traced here: 70.9 us
  blocking collectives  60.1 us (84%)
  Pallas kernels  10.1 us (14%)
    all_to_all x3, blocking collectives, packed_shards(): got = lax.all_to_all(part, AXES, 0, 0, tiled=True)  31.2 us
    all_to_all x1, blocking collectives, packed_shards(): got = lax.all_to_all(send, AXES, 0, 0, tiled=True)  29 us
    pallas_call x1, Pallas kernels, packed_shards(): pl.pallas_call(bind(assemble_kernel), out_shape=(jax.ShapeDtypeStruct((de...  6.49 us
    pallas_call x2, Pallas kernels, packed_shards(): pl.pallas_call(bind(step_kernel, begin), out_shape=outs, in_specs=[vmem()...  2.17 us

profile of v7, /device:TPU:0, one launch (start us, length us, event | category | flops | bytes accessed | tf_op | source)
XLA Modules:
  0.0 70.9 jit_solution(9853892253271635989)
XLA Ops:
  0.6 6.5 %assemble.1 = (bf16[32,96,128]{2,1,0:T(8,128)(2,1)S(1)}, bf16[256,256]{1,0:T(8,128)(2,1)S(1)}) custom-call(bf16[2,2,6,16,1024]{4,3,2,1,0:T(8,128)(2,1)} %refs_0_.1, bf16[2,2,3,16,1024]{4,3,2,1,0:T(8,128)(2,1)} %refs_1_.1, bf16[2,2,16,1024]{3,2,1,0:T(8,128)(2,1)} %refs_2_.1, s32[16,1024]{1,0:T(8,128)} %refs_3_.1, s32[1,512]{1,0:T(1,128)} %bitcast.4, ...), custom_call_target="tpu_custom_call" | custom-call | tf_op jit(solution)/shard_map/assemble/pallas_call | solution.py:498
  7.1 29.0 %all_to_all.20.refs_0_ = bf16[32,96,128]{2,1,0:T(8,128)(2,1)S(1)} all-to-all(bf16[32,96,128]{2,1,0:T(8,128)(2,1)S(1)} %get-tuple-element.15), channel_id=1, replica_groups=mesh['row'=4,'col'=8] {'row','col'}, dimensions={0} | all-to-all | bytes 1572864 | tf_op jit(solution)/shard_map/all_to_all | solution.py:532
  36.1 0.6 first.1
  36.7 10.6 %all_to_all.21.refs_0_ = f32[32,1,1280]{2,1,0:T(1,128)S(1)} all-to-all(f32[32,1,1280]{2,1,0:T(1,128)S(1)} %get-tuple-element.17), channel_id=1, replica_groups=mesh['row'=4,'col'=8] {'row','col'}, dimensions={0} | all-to-all | bytes 327680 | tf_op jit(solution)/shard_map/all_to_all | solution.py:548
  47.4 1.4 %step.2 = (f32[3,4,8,128]{3,2,1,0:T(8,128)S(1)}, f32[32,1,1152]{2,1,0:T(1,128)S(1)}, bf16[36,64,128]{2,1,0:T(8,128)(2,1)}) custom-call(f32[32,1,1280]{2,1,0:T(1,128)S(1)} %all_to_all.21.refs_0_, bf16[36,64,128]{2,1,0:T(8,128)(2,1)S(1)} %get-tuple-element.18.refs_1_, f32[8,128]{1,0:T(8,128)S(1)} %get-tuple-element.19.refs_2_, ...), custom_call_target="tpu_custom_call" | custom-call | tf_op jit(solution)/shard_map/step/pallas_call | solution.py:560
  48.8 10.4 %all_to_all.22.refs_0_ = f32[32,1,1152]{2,1,0:T(1,128)S(1)} all-to-all(f32[32,1,1152]{2,1,0:T(1,128)S(1)} %get-tuple-element.21), channel_id=1, replica_groups=mesh['row'=4,'col'=8] {'row','col'}, dimensions={0} | all-to-all | bytes 294912 | tf_op jit(solution)/shard_map/all_to_all | solution.py:548
  59.1 0.8 %step.3 = (f32[3,4,8,128]{3,2,1,0:T(8,128)S(1)}, f32[32,1,1152]{2,1,0:T(1,128)S(1)}) custom-call(f32[32,1,1152]{2,1,0:T(1,128)S(1)} %all_to_all.22.refs_0_, bf16[36,64,128]{2,1,0:T(8,128)(2,1)S(1)} %get-tuple-element.18.refs_1_, f32[8,128]{1,0:T(8,128)S(1)} %get-tuple-element.19.refs_2_, f32[3,4,8,128]{3,2,1,0:T(8,128)S(1)} %get-tuple-element.22.refs_3_), custom_call_target="tpu_custom_call" | custom-call | tf_op jit(solution)/shard_map/step/pallas_call | solution.py:560
  59.9 10.2 %all_to_all.23.refs_0_ = f32[32,1,1152]{2,1,0:T(1,128)S(1)} all-to-all(f32[32,1,1152]{2,1,0:T(1,128)S(1)} %get-tuple-element.23), channel_id=1, replica_groups=mesh['row'=4,'col'=8] {'row','col'}, dimensions={0} | all-to-all | bytes 294912 | tf_op jit(solution)/shard_map/all_to_all | solution.py:571
  70.1 0.8 %last.1 = (f32[6,128]{1,0:T(8,128)}, f32[6,128]{1,0:T(8,128)}) custom-call(f32[32,1,1152]{2,1,0:T(1,128)S(1)} %all_to_all.23.refs_0_, f32[3,4,8,128]{3,2,1,0:T(8,128)S(1)} %get-tuple-element.24.refs_1_), custom_call_target="tpu_custom_call" | custom-call | tf_op jit(solution)/shard_map/last/pallas_call | solution.py:572
  (1 shorter events, 0.0 us)
